TPU v7x, 128 devices: a whole 4x4x4 slice. The times are simulated.
128 devices in a mesh: wide: 16 (over z, x_lo, core), narrow: 8 (over y, x_hi).
Axes of the slice: x: 4 (x_hi: 2, x_lo: 2; x = x_hi * 2 + x_lo), y: 4, z: 4, core: 2. Of those that a mesh axis runs over, the one named last changes fastest.
Arguments:
- offsets: float32 [2, 16, 8, 8192], P(None, 'wide', 'narrow'), may hold values from -1 to 1
- strengths: float32 [2, 16, 8, 8192], P(None, 'wide', 'narrow'), may hold values from -1.2 to 1.2
- leaf_map: int32 [16, 8, 8192], P('wide', 'narrow'), may hold values from 0 to 1023
- shift_matrices: float32 [7, 4, 128, 128], replicated, may hold values from -0.25 to 0.25
- transfer_diagonal: float32 [5, 49, 128], replicated, may hold values from -1.25 to 1.25
Outputs:
- leaf_multipoles: float32 [512, 256, 128], P('wide', 'narrow')
- local_zero: float32 [16, 8, 128], P('wide', 'narrow')
- local_one: float32 [32, 16, 128], P('wide', 'narrow')
- local_two: float32 [64, 32, 128], P('wide', 'narrow')
- local_three: float32 [128, 64, 128], P('wide', 'narrow')
- coarse_local: float32 [8, 4, 128], replicated
- top_multipole: float32 [4, 2, 128], replicated
All inputs are finite; a program needn't handle non-finite values.
Results may differ from a plain program's by a relative error of at most 0.0003.
Values sent between devices are 32-bit elements; how exact they have to be, the bound alone decides.
No kernel may reach another device: no remote copies, remote signals or barrier semaphores. Data moves between devices by JAX's collectives and lax.ppermute only.
A program may use at most 128 MiB of HBM per device.

v0:
```python
import math

import jax
import jax.numpy as jnp
from jax import lax
from jax.sharding import Mesh
from jax.sharding import PartitionSpec as P

ORDER = 64
LOCAL = 5
COARSE = 2
LEAF_SIDE = 32
NARROW = ("narrow_0", "narrow_1")


HIGHEST = lax.Precision.HIGHEST


def whole_of(shard, axes, dim):
    for axis in reversed(axes):
        shard = lax.all_gather(shard, axis, axis=dim, tiled=True)
    return shard


def joined_along(tiles, dim):
    dims = list(tiles.shape[1:])
    dims[dim] *= tiles.shape[0]
    return jnp.moveaxis(tiles, 0, dim).reshape(dims)


def gather_packed(arrays, axis, dims):
    vector = jnp.concatenate([a.reshape(-1) for a in arrays])
    lines, at, outs = (lax.all_gather(vector, axis), 0, [])
    for a, dim in zip(arrays, dims):
        tiles = lines[:, at : at + a.size].reshape(-1, *a.shape)
        outs.append(joined_along(tiles, dim))
        at += a.size
    return tuple(outs)


def padded_2(cells, sides, width):
    for axis, dim in sides:
        count = lax.axis_size(axis)
        ends = count - 1
        head = lax.slice_in_dim(cells, 0, width, axis=dim)
        tail = lax.slice_in_dim(cells, cells.shape[dim] - width, cells.shape[dim], axis=dim)
        cells = jnp.concatenate(
            [
                lax.ppermute(tail, axis, [(i, (i + 1) % count) for i in range(ends)]),
                cells,
                lax.ppermute(head, axis, [((i + 1) % count, i) for i in range(ends)]),
            ],
            axis=dim,
        )
    return cells


def panel_terms(coords, charge):
    degree = jnp.arange(ORDER).astype(jnp.float32)
    cheb_first = jnp.cos(degree[None, :] * jnp.arccos(coords[0])[:, None])
    cheb_second = jnp.cos(degree[None, :] * jnp.arccos(coords[1])[:, None])
    real_part = charge[0][:, None] * cheb_first - charge[1][:, None] * cheb_second
    imag_part = charge[0][:, None] * cheb_second + charge[1][:, None] * cheb_first
    return jnp.concatenate([real_part, imag_part], axis=1)


def merge_children(children, operators):
    row_count, col_count, coeff_width = children.shape
    grouped = children.reshape(row_count // 2, 2, col_count // 2, 2, coeff_width)
    parent = jnp.zeros((row_count // 2 * (col_count // 2), coeff_width), jnp.float32)
    for row_bit in range(2):
        for col_bit in range(2):
            quarter = grouped[:, row_bit, :, col_bit, :].reshape(-1, coeff_width)
            parent = parent + jnp.dot(
                quarter,
                operators[2 * row_bit + col_bit],
                precision=HIGHEST,
                preferred_element_type=jnp.float32,
            )
    return parent.reshape(row_count // 2, col_count // 2, coeff_width)


def transfer(padded, diagonal, row_start, col_start, row_count, col_count):
    half_width = diagonal.shape[1] // 2
    row_parity = (row_start + jnp.arange(row_count, dtype=jnp.int32)) % 2
    col_parity = (col_start + jnp.arange(col_count, dtype=jnp.int32)) % 2
    summed = jnp.zeros((row_count, col_count, diagonal.shape[1]), jnp.float32)
    for shift_row in range(-3, 4):
        for shift_col in range(-3, 4):
            if max(abs(shift_row), abs(shift_col)) < 2:
                continue
            row_ok = ((shift_row >= -2 - row_parity) & (shift_row <= 3 - row_parity)).astype(
                jnp.float32
            )
            col_ok = ((shift_col >= -2 - col_parity) & (shift_col <= 3 - col_parity)).astype(
                jnp.float32
            )
            allowed = row_ok[:, None] * col_ok[None, :]
            source = padded[
                3 + shift_row : 3 + shift_row + row_count,
                3 + shift_col : 3 + shift_col + col_count,
                :,
            ]
            factor = diagonal[(shift_row + 3) * 7 + shift_col + 3]
            diag_real = factor[:half_width]
            diag_imag = factor[half_width:]
            src_real = source[..., :half_width]
            src_imag = source[..., half_width:]
            product = jnp.concatenate(
                [
                    diag_real * src_real - diag_imag * src_imag,
                    diag_real * src_imag + diag_imag * src_real,
                ],
                axis=-1,
            )
            summed = summed + allowed[:, :, None] * product
    return summed


def pad_grid(current):
    return jnp.pad(current, ((3, 3), (3, 3), (0, 0)))


def gather_top(pieces):
    along_row = (whole_of(pieces[0], NARROW, 1), whole_of(pieces[1], NARROW, 1))
    result = gather_packed((along_row[0], along_row[1]), "wide", (0, 0))
    return result


def own_region(whole, box_side, wide_at, narrow_at):
    coeff_width = whole.shape[2]
    return lax.dynamic_slice(
        pad_grid(whole),
        (wide_at * box_side, narrow_at * box_side, jnp.int32(0)),
        (box_side + 6, box_side + 6, coeff_width),
    )


def local(offsets, strengths, leaf_map, shift_matrices, transfer_diagonal):
    flat_coords = offsets.reshape(2, -1)
    flat_charge = strengths.reshape(2, -1)
    leaves = leaf_map.reshape(-1)
    panel_count = flat_coords.shape[1]
    block_size = math.gcd(panel_count, 2048)
    block_count = panel_count // block_size
    leaf_count = LEAF_SIDE * LEAF_SIDE
    leaf_ids = jnp.arange(leaf_count, dtype=jnp.int32)

    def add_block(totals, number):
        begin = number * block_size
        coords = lax.dynamic_slice_in_dim(flat_coords, begin, block_size, 1)
        charge = lax.dynamic_slice_in_dim(flat_charge, begin, block_size, 1)
        pieces = lax.dynamic_slice_in_dim(leaves, begin, block_size, 0)
        selector = (leaf_ids[:, None] == pieces[None, :]).astype(jnp.float32)
        return (
            totals
            + jnp.dot(
                selector,
                panel_terms(coords, charge),
                precision=HIGHEST,
                preferred_element_type=jnp.float32,
            ),
            None,
        )

    totals, _ = lax.scan(
        add_block,
        jnp.zeros((leaf_count, 2 * ORDER), jnp.float32),
        jnp.arange(block_count, dtype=jnp.int32),
    )
    leaf_grid = totals.reshape(LEAF_SIDE, LEAF_SIDE, 2 * ORDER)
    levels = {LOCAL: leaf_grid}
    for level in range(LOCAL - 1, -1, -1):
        levels[level] = merge_children(levels[level + 1], shift_matrices[COARSE + level])
    wide_at = lax.axis_index("wide")
    narrow_at = lax.axis_index(NARROW)
    whole_zero, whole_one = gather_top((levels[0], levels[1]))
    regions = []
    for level in (2, 3):
        regions.append(padded_2(levels[level], (("wide", 0), (NARROW, 1)), 3))
    region_two = regions[0]
    region_three = regions[1]
    coarse_grid = merge_children(whole_zero, shift_matrices[1])
    top_grid = merge_children(coarse_grid, shift_matrices[0])
    coarse_local = transfer(
        pad_grid(coarse_grid),
        transfer_diagonal[0],
        0,
        0,
        coarse_grid.shape[0],
        coarse_grid.shape[1],
    )
    region_zero = own_region(whole_zero, 1, wide_at, narrow_at)
    local_zero = transfer(region_zero, transfer_diagonal[1], wide_at, narrow_at, 1, 1)
    region_one = own_region(whole_one, 2, wide_at, narrow_at)
    local_one = transfer(region_one, transfer_diagonal[2], wide_at * 2, narrow_at * 2, 2, 2)
    local_two = transfer(region_two, transfer_diagonal[3], wide_at * 4, narrow_at * 4, 4, 4)
    local_three = transfer(region_three, transfer_diagonal[4], wide_at * 8, narrow_at * 8, 8, 8)
    return (leaf_grid, local_zero, local_one, local_two, local_three, coarse_local, top_grid)


def solution(mesh):
    split = Mesh(mesh.devices.reshape(mesh.shape["wide"], 4, 2), ("wide", "narrow_0", "narrow_1"))
    return jax.shard_map(
        local,
        mesh=split,
        in_specs=(
            P(None, "wide", NARROW, None),
            P(None, "wide", NARROW, None),
            P("wide", NARROW, None),
            P(),
            P(),
        ),
        out_specs=(
            P("wide", NARROW, None),
            P("wide", NARROW, None),
            P("wide", NARROW, None),
            P("wide", NARROW, None),
            P("wide", NARROW, None),
            P(),
            P(),
        ),
        check_vma=False,
    )
```

profile of v0, /device:TPU:0, one launch (start us, length us, event | category | flops | bytes accessed | tf_op | source)
XLA Modules:
  0.0 204.9 jit_solution(366430313679942541)
XLA Ops:
  1.6 39.0 %while.11 = (s32[]{:T(128)}, f32[1024,128]{1,0:T(8,128)S(1)}, s32[4]{0:T(128)S(1)}, s32[8192]{0:T(1024)}, f32[2,8192]{1,0:T(2,128)S(1)}, /*index=5*/f32[2,8192]{...) while((s32[]{:T(128)}, f32[1024,128]{1,0:T(8,128)S(1)}, ...), condition=%wide.region_1.2_spmd.clone, body=%wide.region_0.1_spmd.clone.sunk | while | flops 3224907776 | bytes 3302097 | solution.py:166
  3.8 3.5 %multiply_subtract_fusion.202 = (f32[2048,64]{0,1:T(8,128)S(1)}, f32[2048,64]{0,1:T(8,128)S(1)}) fusion(f32[2048]{0:T(1024)S(1)} %sqrt_atan2_fusion.4, f32[2048]{0:T(1024)S(1)} %bitcast.932, f32[2048]{0:T(1024)S(1)} %sqrt_atan2_fusion.5, f32[64]{0:T(128)S(1)} %iota_convert_fusion.2, f32[2048]{0:T(1024)S(1)} %bitcast.931), kind=kLoop, calls=%fused_computation.9.clone.1 | loop fusion | flops 1048576 | bytes 1081600 | tf_op jit(solution)/shard_map/while/body/eval_jaxpr/sub | solution.py:62
  7.3 4.1 %fusion.333 = f32[1024,128]{1,0:T(8,128)S(1)} fusion(s32[2048]{0:T(1024)S(1)} %dynamic_slice.28, f32[2048,64]{0,1:T(8,128)S(1)} %get-tuple-element.1549, f32[2048,64]{0,1:T(8,128)S(1)} %get-tuple-element.1550, f32[1024,128]{1,0:T(8,128)S(1)} %get-tuple-element.1563, pred[]{:T(512)S(6)} %compare.106), kind=kOutput, calls=%fused_computation.4.clone.1 | convolution fusion | flops 3223846912 | bytes 2105345 | tf_op jit(solution)/shard_map/while/body/eval_jaxpr/dot_general | solution.py:157
  13.6 3.5 %multiply_subtract_fusion.202 = (f32[2048,64]{0,1:T(8,128)S(1)}, f32[2048,64]{0,1:T(8,128)S(1)}) fusion(f32[2048]{0:T(1024)S(1)} %sqrt_atan2_fusion.4, f32[2048]{0:T(1024)S(1)} %bitcast.932, f32[2048]{0:T(1024)S(1)} %sqrt_atan2_fusion.5, f32[64]{0:T(128)S(1)} %iota_convert_fusion.2, f32[2048]{0:T(1024)S(1)} %bitcast.931), kind=kLoop, calls=%fused_computation.9.clone.1 | loop fusion | flops 1048576 | bytes 1081600 | tf_op jit(solution)/shard_map/while/body/eval_jaxpr/sub | solution.py:62
  17.1 4.1 %fusion.333 = f32[1024,128]{1,0:T(8,128)S(1)} fusion(s32[2048]{0:T(1024)S(1)} %dynamic_slice.28, f32[2048,64]{0,1:T(8,128)S(1)} %get-tuple-element.1549, f32[2048,64]{0,1:T(8,128)S(1)} %get-tuple-element.1550, f32[1024,128]{1,0:T(8,128)S(1)} %get-tuple-element.1563, pred[]{:T(512)S(6)} %compare.106), kind=kOutput, calls=%fused_computation.4.clone.1 | convolution fusion | flops 3223846912 | bytes 2105345 | tf_op jit(solution)/shard_map/while/body/eval_jaxpr/dot_general | solution.py:157
  23.3 3.5 %multiply_subtract_fusion.202 = (f32[2048,64]{0,1:T(8,128)S(1)}, f32[2048,64]{0,1:T(8,128)S(1)}) fusion(f32[2048]{0:T(1024)S(1)} %sqrt_atan2_fusion.4, f32[2048]{0:T(1024)S(1)} %bitcast.932, f32[2048]{0:T(1024)S(1)} %sqrt_atan2_fusion.5, f32[64]{0:T(128)S(1)} %iota_convert_fusion.2, f32[2048]{0:T(1024)S(1)} %bitcast.931), kind=kLoop, calls=%fused_computation.9.clone.1 | loop fusion | flops 1048576 | bytes 1081600 | tf_op jit(solution)/shard_map/while/body/eval_jaxpr/sub | solution.py:62
  26.8 4.1 %fusion.333 = f32[1024,128]{1,0:T(8,128)S(1)} fusion(s32[2048]{0:T(1024)S(1)} %dynamic_slice.28, f32[2048,64]{0,1:T(8,128)S(1)} %get-tuple-element.1549, f32[2048,64]{0,1:T(8,128)S(1)} %get-tuple-element.1550, f32[1024,128]{1,0:T(8,128)S(1)} %get-tuple-element.1563, pred[]{:T(512)S(6)} %compare.106), kind=kOutput, calls=%fused_computation.4.clone.1 | convolution fusion | flops 3223846912 | bytes 2105345 | tf_op jit(solution)/shard_map/while/body/eval_jaxpr/dot_general | solution.py:157
  33.0 3.5 %multiply_subtract_fusion.202 = (f32[2048,64]{0,1:T(8,128)S(1)}, f32[2048,64]{0,1:T(8,128)S(1)}) fusion(f32[2048]{0:T(1024)S(1)} %sqrt_atan2_fusion.4, f32[2048]{0:T(1024)S(1)} %bitcast.932, f32[2048]{0:T(1024)S(1)} %sqrt_atan2_fusion.5, f32[64]{0:T(128)S(1)} %iota_convert_fusion.2, f32[2048]{0:T(1024)S(1)} %bitcast.931), kind=kLoop, calls=%fused_computation.9.clone.1 | loop fusion | flops 1048576 | bytes 1081600 | tf_op jit(solution)/shard_map/while/body/eval_jaxpr/sub | solution.py:62
  36.5 4.1 %fusion.333 = f32[1024,128]{1,0:T(8,128)S(1)} fusion(s32[2048]{0:T(1024)S(1)} %dynamic_slice.28, f32[2048,64]{0,1:T(8,128)S(1)} %get-tuple-element.1549, f32[2048,64]{0,1:T(8,128)S(1)} %get-tuple-element.1550, f32[1024,128]{1,0:T(8,128)S(1)} %get-tuple-element.1563, pred[]{:T(512)S(6)} %compare.106), kind=kOutput, calls=%fused_computation.4.clone.1 | convolution fusion | flops 3223846912 | bytes 2105345 | tf_op jit(solution)/shard_map/while/body/eval_jaxpr/dot_general | solution.py:157
  43.8 1.3 collective-permute-start.1
  45.1 3.0 %collective-permute-start = (f32[3,4,128]{2,1,0:T(4,128)S(1)}, f32[3,4,128]{2,1,0:T(4,128)S(1)}, u32[]{:S(2)}, u32[]{:S(2)}) collective-permute-start(f32[3,4,128]{2,1,0:T(4,128)S(1)} %slice.5136), channel_id=1, source_target_pairs={{0,8},{8,16},{16,24},{24,32},{32,40},{40,48},{48,56},{56,64},{64,7... | collective-permute-start | bytes 18440 | tf_op jit(solution)/shard_map/ppermute | solution.py:49
  48.1 1.3 collective-permute-start.5
  49.4 3.8 %collective-permute-start.4 = (f32[3,8,128]{2,1,0:T(8,128)S(1)}, f32[3,8,128]{2,1,0:T(8,128)S(1)}, u32[]{:S(2)}, u32[]{:S(2)}) collective-permute-start(f32[3,8,128]{2,1,0:T(8,128)S(1)} %get-tuple-element.1114), channel_id=1, source_target_pairs={{0,8},{8,16},{16,24},{24,32},{32,40},{40,48},{48,56},{56,64},{64,7... | collective-permute-start | bytes 36872 | tf_op jit(solution)/shard_map/ppermute | solution.py:49
  53.9 5.9 %all_gather.20 = f32[2,4,128]{2,0,1:T(2,128)S(1)} all-gather(f32[2,2,128]{2,0,1:T(2,128)S(1)} %copy.34), channel_id=1, replica_groups=mesh['wide'=16,'narrow_0'=4,'narrow_1'=2] {'narrow_1'}, dimensions={1}, use_global_device_ids=true | all-gather | bytes 6144 | tf_op jit(solution)/shard_map/all_gather | solution.py:21
  59.8 12.5 %all_gather.21 = f32[2,16,128]{2,0,1:T(2,128)S(1)} all-gather(f32[2,4,128]{2,0,1:T(2,128)S(1)} %all_gather.20), channel_id=1, replica_groups=mesh['wide'=16,'narrow_0'=4,'narrow_1'=2] {'narrow_0'}, dimensions={1}, use_global_device_ids=true | all-gather | bytes 20480 | tf_op jit(solution)/shard_map/all_gather | solution.py:21
  73.0 5.8 %all-gather.2 = f32[2,1,128]{2,1,0:T(1,128)S(1)} all-gather(f32[1,1,128]{2,1,0:T(1,128)S(1)} %fusion.10), channel_id=2, replica_groups=mesh['wide'=16,'narrow_0'=4,'narrow_1'=2] {'narrow_1'}, dimensions={0}, use_global_device_ids=true | all-gather | bytes 1536 | tf_op jit(solution)/shard_map/all_gather | solution.py:21
  78.7 9.5 %all_gather.19 = f32[1,8,128]{2,0,1:T(1,128)S(1)} all-gather(f32[1,2,128]{2,0,1:T(1,128)S(1)} %bitcast.976), channel_id=1, replica_groups=mesh['wide'=16,'narrow_0'=4,'narrow_1'=2] {'narrow_0'}, dimensions={1}, use_global_device_ids=true | all-gather | bytes 5120 | tf_op jit(solution)/shard_map/all_gather | solution.py:21
  88.2 22.5 %all-gather.1 = f32[81920]{0:T(1024)S(1)} all-gather(f32[5120]{0:T(1024)S(1)} %pad_maximum_fusion.5), channel_id=3, replica_groups=mesh['wide'=16,'narrow_0'=4,'narrow_1'=2] {'wide'}, dimensions={0}, use_global_device_ids=true | all-gather | bytes 348160 | tf_op jit(solution)/shard_map/all_gather | solution.py:33
  168.1 1.4 fusion.158
  171.0 1.3 collective-permute-start.3
  172.3 6.1 %collective-permute-start.2 = (f32[10,3,128]{2,1,0:T(4,128)S(1)}, f32[10,3,128]{2,1,0:T(4,128)S(1)}, u32[]{:S(2)}, u32[]{:S(2)}) collective-permute-start(f32[10,3,128]{2,1,0:T(4,128)S(1)} %get-tuple-element.1123), channel_id=1, source_target_pairs={{0,1},{1,2},{2,3},{3,4},{4,5},{5,6},{6,7},{8,9},{9,10},{10,11},{11... | collective-permute-start | bytes 46088 | tf_op jit(solution)/shard_map/ppermute | solution.py:49
  179.9 5.8 %collective-permute-start.6 = (f32[14,3,128]{2,1,0:T(4,128)S(1)}, f32[14,3,128]{2,1,0:T(4,128)S(1)}, u32[]{:S(2)}, u32[]{:S(2)}) collective-permute-start(f32[14,3,128]{2,1,0:T(4,128)S(1)} %get-tuple-element.980), channel_id=1, source_target_pairs={{0,1},{1,2},{2,3},{3,4},{4,5},{5,6},{6,7},{8,9},{9,10},{10,11},{11... | collective-permute-start | bytes 64520 | tf_op jit(solution)/shard_map/ppermute | solution.py:49
  185.7 1.5 collective-permute-start.7
  203.2 1.6 fusion.119
  (567 shorter events, 84.8 us)
Async XLA Ops:
  1.6 39.4 %copy-start = (f32[7,4,128,128]{3,2,1,0:T(8,128)S(1)}, f32[7,4,128,128]{3,2,1,0:T(8,128)}, u32[]{:S(2)}) copy-start(f32[7,4,128,128]{3,2,1,0:T(8,128)} %param.10) | copy-start | bytes 5505028
  42.1 68.7 %copy-start.2 = (f32[5,49,128]{2,1,0:T(8,128)S(1)}, f32[5,49,128]{2,1,0:T(8,128)}, u32[]{:S(2)}) copy-start(f32[5,49,128]{2,1,0:T(8,128)} %param.11) | copy-start | bytes 376324
  43.8 126.9 %collective-permute-start.1 = (f32[3,4,128]{2,1,0:T(4,128)S(1)}, f32[3,4,128]{2,1,0:T(4,128)S(1)}, u32[]{:S(2)}, u32[]{:S(2)}) collective-permute-start(f32[3,4,128]{2,1,0:T(4,128)S(1)} %slice.5138), channel_id=1, source_target_pairs={{8,0},{16,8},{24,16},{32,24},{40,32},{48,40},{56,48},{64,56},{72,6... | collective-permute-start | bytes 18440 | tf_op jit(solution)/shard_map/ppermute | solution.py:51
  45.1 125.8 %collective-permute-start = (f32[3,4,128]{2,1,0:T(4,128)S(1)}, f32[3,4,128]{2,1,0:T(4,128)S(1)}, u32[]{:S(2)}, u32[]{:S(2)}) collective-permute-start(f32[3,4,128]{2,1,0:T(4,128)S(1)} %slice.5136), channel_id=1, source_target_pairs={{0,8},{8,16},{16,24},{24,32},{32,40},{40,48},{48,56},{56,64},{64,7... | collective-permute-start | bytes 18440 | tf_op jit(solution)/shard_map/ppermute | solution.py:49
  48.1 131.7 %collective-permute-start.5 = (f32[3,8,128]{2,1,0:T(8,128)S(1)}, f32[3,8,128]{2,1,0:T(8,128)S(1)}, u32[]{:S(2)}, u32[]{:S(2)}) collective-permute-start(f32[3,8,128]{2,1,0:T(8,128)S(1)} %get-tuple-element.1115), channel_id=1, source_target_pairs={{8,0},{16,8},{24,16},{32,24},{40,32},{48,40},{56,48},{64,56},{72,6... | collective-permute-start | bytes 36872 | tf_op jit(solution)/shard_map/ppermute | solution.py:51
  49.4 130.4 %collective-permute-start.4 = (f32[3,8,128]{2,1,0:T(8,128)S(1)}, f32[3,8,128]{2,1,0:T(8,128)S(1)}, u32[]{:S(2)}, u32[]{:S(2)}) collective-permute-start(f32[3,8,128]{2,1,0:T(8,128)S(1)} %get-tuple-element.1114), channel_id=1, source_target_pairs={{0,8},{8,16},{16,24},{24,32},{32,40},{40,48},{48,56},{56,64},{64,7... | collective-permute-start | bytes 36872 | tf_op jit(solution)/shard_map/ppermute | solution.py:49
  170.7 24.8 %copy-start.108 = (f32[64]{0:T(128)S(1)}, f32[64]{0:T(128)}, u32[]{:S(2)}) copy-start(f32[64]{0:T(128)} %get-tuple-element.733) | copy-start | bytes 772
  170.7 24.8 %copy-start.109 = (f32[64]{0:T(128)S(1)}, f32[64]{0:T(128)}, u32[]{:S(2)}) copy-start(f32[64]{0:T(128)} %get-tuple-element.734) | copy-start | bytes 772
  170.8 24.8 %copy-start.84 = (f32[64]{0:T(128)S(1)}, f32[64]{0:T(128)}, u32[]{:S(2)}) copy-start(f32[64]{0:T(128)} %get-tuple-element.750) | copy-start | bytes 772
  170.8 24.8 %copy-start.85 = (f32[64]{0:T(128)S(1)}, f32[64]{0:T(128)}, u32[]{:S(2)}) copy-start(f32[64]{0:T(128)} %get-tuple-element.751) | copy-start | bytes 772
  170.8 24.8 %copy-start.104 = (f32[64]{0:T(128)S(1)}, f32[64]{0:T(128)}, u32[]{:S(2)}) copy-start(f32[64]{0:T(128)} %get-tuple-element.737) | copy-start | bytes 772
  170.8 24.8 %copy-start.105 = (f32[64]{0:T(128)S(1)}, f32[64]{0:T(128)}, u32[]{:S(2)}) copy-start(f32[64]{0:T(128)} %get-tuple-element.738) | copy-start | bytes 772
  170.8 24.8 %copy-start.106 = (f32[64]{0:T(128)S(1)}, f32[64]{0:T(128)}, u32[]{:S(2)}) copy-start(f32[64]{0:T(128)} %get-tuple-element.739) | copy-start | bytes 772
  170.8 24.8 %copy-start.107 = (f32[64]{0:T(128)S(1)}, f32[64]{0:T(128)}, u32[]{:S(2)}) copy-start(f32[64]{0:T(128)} %get-tuple-element.740) | copy-start | bytes 772
  170.9 26.3 %copy-start.74 = (f32[64]{0:T(128)S(1)}, f32[64]{0:T(128)}, u32[]{:S(2)}) copy-start(f32[64]{0:T(128)} %get-tuple-element.629) | copy-start | bytes 772
  170.9 26.3 %copy-start.75 = (f32[64]{0:T(128)S(1)}, f32[64]{0:T(128)}, u32[]{:S(2)}) copy-start(f32[64]{0:T(128)} %get-tuple-element.630) | copy-start | bytes 772
  170.9 26.3 %copy-start.95 = (f32[64]{0:T(128)S(1)}, f32[64]{0:T(128)}, u32[]{:S(2)}) copy-start(f32[64]{0:T(128)} %get-tuple-element.650) | copy-start | bytes 772
  170.9 26.3 %copy-start.96 = (f32[64]{0:T(128)S(1)}, f32[64]{0:T(128)}, u32[]{:S(2)}) copy-start(f32[64]{0:T(128)} %get-tuple-element.651) | copy-start | bytes 772
  170.9 26.3 %copy-start.97 = (f32[64]{0:T(128)S(1)}, f32[64]{0:T(128)}, u32[]{:S(2)}) copy-start(f32[64]{0:T(128)} %get-tuple-element.652) | copy-start | bytes 772
  170.9 26.3 %copy-start.98 = (f32[64]{0:T(128)S(1)}, f32[64]{0:T(128)}, u32[]{:S(2)}) copy-start(f32[64]{0:T(128)} %get-tuple-element.653) | copy-start | bytes 772
  171.0 17.8 %collective-permute-start.3 = (f32[10,3,128]{2,1,0:T(4,128)S(1)}, f32[10,3,128]{2,1,0:T(4,128)S(1)}, u32[]{:S(2)}, u32[]{:S(2)}) collective-permute-start(f32[10,3,128]{2,1,0:T(4,128)S(1)} %get-tuple-element.1122), channel_id=1, source_target_pairs={{1,0},{2,1},{3,2},{4,3},{5,4},{6,5},{7,6},{9,8},{10,9},{11,10},{12... | collective-permute-start | bytes 46088 | tf_op jit(solution)/shard_map/ppermute | solution.py:51
  172.3 16.5 %collective-permute-start.2 = (f32[10,3,128]{2,1,0:T(4,128)S(1)}, f32[10,3,128]{2,1,0:T(4,128)S(1)}, u32[]{:S(2)}, u32[]{:S(2)}) collective-permute-start(f32[10,3,128]{2,1,0:T(4,128)S(1)} %get-tuple-element.1123), channel_id=1, source_target_pairs={{0,1},{1,2},{2,3},{3,4},{4,5},{5,6},{6,7},{8,9},{9,10},{10,11},{11... | collective-permute-start | bytes 46088 | tf_op jit(solution)/shard_map/ppermute | solution.py:49
  179.9 17.2 %collective-permute-start.6 = (f32[14,3,128]{2,1,0:T(4,128)S(1)}, f32[14,3,128]{2,1,0:T(4,128)S(1)}, u32[]{:S(2)}, u32[]{:S(2)}) collective-permute-start(f32[14,3,128]{2,1,0:T(4,128)S(1)} %get-tuple-element.980), channel_id=1, source_target_pairs={{0,1},{1,2},{2,3},{3,4},{4,5},{5,6},{6,7},{8,9},{9,10},{10,11},{11... | collective-permute-start | bytes 64520 | tf_op jit(solution)/shard_map/ppermute | solution.py:49
  185.7 11.4 %collective-permute-start.7 = (f32[14,3,128]{2,1,0:T(4,128)S(1)}, f32[14,3,128]{2,1,0:T(4,128)S(1)}, u32[]{:S(2)}, u32[]{:S(2)}) collective-permute-start(f32[14,3,128]{2,1,0:T(4,128)S(1)} %get-tuple-element.981), channel_id=1, source_target_pairs={{1,0},{2,1},{3,2},{4,3},{5,4},{6,5},{7,6},{9,8},{10,9},{11,10},{12... | collective-permute-start | bytes 64520 | tf_op jit(solution)/shard_map/ppermute | solution.py:51
  (139 other events, 1280.1 us)
where the time goes:
time: 207 us; the launch traced here: 205 us
  other arithmetic  78.6 us (38%)
  blocking collectives  56.1 us (27%)
  starting transfers between devices  24 us (12%)
  matrix products  21.9 us (11%)
  local copies, waits for them, and re-layouts  17.5 us (8%)
  between operations  3.87 us (2%)
  loops' own time  2.86 us (1%)
    all_gather x4, blocking collectives, whole_of(): shard = lax.all_gather(shard, axis, axis=dim, tiled=True)  33.6 us
    sub x66, other arithmetic, transfer(): diag_real * src_real - diag_imag * src_imag  32.2 us
    all_gather x1, blocking collectives, gather_packed(): lines, at, outs = (lax.all_gather(vector, axis), 0, [])  22.5 us
    ppermute x4, starting transfers between devices, padded_2(): lax.ppermute(tail, axis, [(i, (i + 1) % count) for i in range(ends)])  18.6 us
    dot_general x4, matrix products, add_block(): jnp.dot(selector, panel_terms(coords, charge), precision=HIGHEST, preferr...  16.2 us
    sub x4, other arithmetic, panel_terms(): charge[0][:, None] * cheb_first - charge[1][:, None] * cheb_second  13.9 us
    convert_element_type x15, other arithmetic, transfer(): ((shift_row >= -2 - row_parity) & (shift_row <= 3 - row_parity)).astype(j...  8.48 us
    convert_element_type x14, other arithmetic, transfer(): ((shift_col >= -2 - col_parity) & (shift_col <= 3 - col_parity)).astype(j...  7.79 us
  transfers between devices with their start and end apart: 8, of which 0 were waited for; matrix products, arithmetic and copies ran while one was open for 34% of the time, Pallas kernels for 0%

commit v1 on v0

v1 whole, which is shorter than its diff:
```python
import functools

import jax
import jax.numpy as jnp
from jax import lax
from jax.experimental import pallas as pl
from jax.experimental.pallas import tpu as pltpu
from jax.sharding import PartitionSpec as P

LANES = 128
GROUPS = 64
LEAVES = 1024
ALL = ("wide", "narrow")
F32 = jnp.float32
BF16 = jnp.bfloat16
VMEM = pl.BlockSpec(memory_space=pltpu.VMEM)
ANY = pl.BlockSpec(memory_space=pl.ANY)
HALO_ROWS = 28
HALO_COLS = 52


def split_weights(src, dst):
    for quarter in range(4):
        rows = slice(quarter * 128, (quarter + 1) * 128)
        w = src[quarter]
        high = w.astype(BF16)
        dst[rows, 0:128] = high
        dst[rows, 128:256] = (w - high.astype(F32)).astype(BF16)


def merge(x, weights):
    count = x.shape[0]
    high = x.astype(BF16).astype(F32)
    both = jnp.concatenate([high, x - high], axis=0).astype(BF16)
    y = jnp.dot(both, weights, preferred_element_type=F32)
    return y[:count, :128] + y[:count, 128:] + y[count:, :128] + y[count:, 128:]


def gather_children(src, dst, rows, cols):
    for row_bit in range(2):
        for col_bit in range(2):
            quarter = 2 * row_bit + col_bit
            lanes = slice(quarter * 128, (quarter + 1) * 128)
            for r in range(rows):
                start = (2 * r + row_bit) * 2 * cols + col_bit
                if cols > 1:
                    piece = src[pl.ds(start, cols, stride=2), :]
                else:
                    piece = src[start : start + 1, :]
                dst[r * cols : (r + 1) * cols, lanes] = piece


def up_kernel(
    off, strg, lmap, shifts,
    leaf_out, l3_out, l2_out, l1_out, l0_out, up_out, down_out,
    cheb, back, terms, acc, leaf, w_raw, w_two, x4, l4, x3, x2, x1, x0, w_sem, o_sem,
):
    w_copy = pltpu.make_async_copy(shifts.at[pl.ds(2, 5)], w_raw, w_sem)
    w_copy.start()

    for i in range(2):
        a = off[i]
        t = [None] * 9
        t[0] = jnp.ones_like(a)
        t[1] = a
        t[2] = 2.0 * a * a - 1.0
        t[3] = 2.0 * t[2] * a - a
        t[4] = 2.0 * t[2] * t[2] - 1.0
        t[5] = 2.0 * t[3] * t[2] - a
        t[6] = 2.0 * t[3] * t[3] - 1.0
        t[7] = 2.0 * t[4] * t[3] - a
        t[8] = 2.0 * t[4] * t[4] - 1.0
        for j in range(9):
            cheb[i, j * GROUPS : (j + 1) * GROUPS, :] = t[j]
        for j in range(8):
            back[i, j * GROUPS : (j + 1) * GROUPS, :] = t[8 - j]

    def make_terms(g, carry):
        blocks = []
        for i in range(2):
            now = cheb[i, pl.ds(g, 8, stride=GROUPS), :]
            before = back[i, pl.ds(g, 8, stride=GROUPS), :]
            twice = 2.0 * jnp.broadcast_to(cheb[i, pl.ds(8 * GROUPS + g, 1), :], (8, LANES))
            seq = [now]
            for _ in range(7):
                now, before = twice * now - before, now
                seq.append(now)
            blocks.append(seq)
        qr = jnp.broadcast_to(strg[0, pl.ds(g, 1), :], (8, LANES))
        qi = jnp.broadcast_to(strg[1, pl.ds(g, 1), :], (8, LANES))
        real = jnp.concatenate([qr * ca - qi * cb for ca, cb in zip(*blocks)], axis=0)
        imag = jnp.concatenate([qr * cb + qi * ca for ca, cb in zip(*blocks)], axis=0)
        whole = jnp.concatenate([real, imag], axis=0)
        high = whole.astype(BF16)
        terms[g, 0:128, :] = high
        terms[g, 128:256, :] = (whole - high.astype(F32)).astype(BF16)
        return carry

    lax.fori_loop(0, GROUPS, make_terms, 0)

    acc[...] = jnp.zeros_like(acc)
    ids = lax.broadcasted_iota(jnp.int32, (256, LANES), 0).astype(F32).astype(BF16)
    one = jnp.ones((256, LANES), BF16)
    zero = jnp.zeros((256, LANES), BF16)

    def add_chunk(k, carry):
        lefts, rights = [], []
        for j in range(8):
            g = k * 8 + j
            row = lmap[pl.ds(g, 1), :]
            parts = []
            for b in range(4):
                near = (row - 256 * b).astype(F32)
                near = jnp.broadcast_to(near, (256, LANES)).astype(BF16)
                parts.append(jnp.where(near == ids, one, zero))
            lefts.append(jnp.concatenate(parts, axis=0))
            rights.append(terms[g])
        left = jnp.concatenate(lefts, axis=1)
        right = jnp.concatenate(rights, axis=1)
        acc[...] += lax.dot_general(
            left, right, (((1,), (1,)), ((), ())), preferred_element_type=F32
        )
        return carry

    lax.fori_loop(0, GROUPS // 8, add_chunk, 0)

    leaf[...] = acc[:, 0:128] + acc[:, 128:256]
    out_copy = pltpu.make_async_copy(leaf, leaf_out, o_sem)
    out_copy.start()
    w_copy.wait()
    for t in range(5):
        split_weights(w_raw.at[t], w_two.at[t])

    gather_children(leaf, x4, 16, 16)
    l4[...] = merge(x4[...], w_two[4])
    gather_children(l4, x3, 8, 8)
    l3_out[...] = merge(x3[...], w_two[3])
    gather_children(l3_out, x2, 4, 4)
    l2_out[...] = merge(x2[...], w_two[2])
    gather_children(l2_out, x1, 2, 2)
    l1_out[...] = merge(x1[...], w_two[1])
    gather_children(l1_out, x0, 1, 1)
    l0_out[...] = jnp.broadcast_to(merge(x0[...], w_two[0])[0:1], (128, LANES))

    up_out[0:16, :] = l3_out[0:16, :]
    up_out[16:24, :] = l2_out[0:8, :]
    up_out[24:28, :] = l1_out[0:4, :]
    down_out[0:16, :] = l3_out[48:64, :]
    down_out[16:24, :] = l2_out[8:16, :]
    down_out[24:28, :] = l1_out[0:4, :]
    out_copy.wait()


def upward(offsets, strengths, leaf_map, shift_matrices):
    shape = lambda *dims: jax.ShapeDtypeStruct(dims, F32)
    scratch = lambda dims, kind=F32: pltpu.VMEM(dims, kind)
    return pl.pallas_call(
        up_kernel,
        out_shape=(
            shape(LEAVES, 128), shape(64, 128), shape(16, 128), shape(8, 128), shape(128, 128),
            shape(HALO_ROWS, 128), shape(HALO_ROWS, 128),
        ),
        in_specs=[VMEM, VMEM, VMEM, ANY],
        out_specs=(ANY,) + (VMEM,) * 6,
        scratch_shapes=[
            scratch((2, 9 * GROUPS, LANES)),
            scratch((2, 8 * GROUPS, LANES)),
            scratch((GROUPS, 256, LANES), BF16),
            scratch((LEAVES, 256)),
            scratch((LEAVES, 128)),
            scratch((5, 4, 128, 128)),
            scratch((5, 512, 256), BF16),
            scratch((256, 512)),
            scratch((256, 128)),
            scratch((64, 512)),
            scratch((16, 512)),
            scratch((8, 512)),
            scratch((8, 512)),
            pltpu.SemaphoreType.DMA,
            pltpu.SemaphoreType.DMA,
        ],
        name="upward",
    )(offsets, strengths, leaf_map, shift_matrices)


LEVELS = ((8, 0, 0), (4, 16, 24), (2, 24, 40))


def pack_kernel(l3, l2, l1, top, bottom, west_out, east_out):
    for grid, (side, row_at, col_at) in zip((l3, l2, l1), LEVELS):
        for out, first in ((west_out, 0), (east_out, side - 2)):
            for k in range(2):
                at = col_at + k * (side + 4)
                c = first + k
                out[at : at + 2, :] = top[pl.ds(row_at + c, 2, stride=side), :]
                out[at + 2 : at + 2 + side, :] = grid[pl.ds(c, side, stride=side), :]
                out[at + 2 + side : at + 4 + side, :] = bottom[pl.ds(row_at + c, 2, stride=side), :]


def pack(l3, l2, l1, top, bottom):
    return pl.pallas_call(
        pack_kernel,
        out_shape=(jax.ShapeDtypeStruct((HALO_COLS, 128), F32),) * 2,
        in_specs=[VMEM] * 5,
        out_specs=(VMEM,) * 2,
        name="pack",
    )(l3, l2, l1, top, bottom)


PITCH = 16


def make_factors(diag, same, cross):
    lane = lax.broadcasted_iota(jnp.int32, (8, LANES), 1)
    for at in (0, 8, 16, 24, 32, 40, 41):
        rows = diag[at : at + 8, :]
        turned = pltpu.roll(rows, 64, 1)
        same[at : at + 8, :] = jnp.where(lane < 64, rows, turned)
        cross[at : at + 8, :] = jnp.where(lane < 64, turned, -rows)


def transfer_rows(region, diag, same, cross, side, cols, store):
    make_factors(diag, same, cross)
    odd = (lax.broadcasted_iota(jnp.int32, (8, LANES), 0) % 2) == 1

    def factor(table, dr, dc):
        at = (dr + 3) * 7 + 3
        if dc < 3:
            return jnp.broadcast_to(table[at + dc : at + dc + 1, :], (8, LANES))
        right = jnp.broadcast_to(table[at + 3 : at + 4, :], (8, LANES))
        left = jnp.broadcast_to(table[at - 3 : at - 2, :], (8, LANES))
        return jnp.where(odd, left, right)

    def source(row, dc):
        base = row * PITCH + 4
        if dc < 3:
            return region[base + dc : base + dc + 8, :]
        return jnp.where(odd, region[base - 3 : base + 5, :], region[base + 3 : base + 11, :])

    for r in range(side):
        first = jnp.zeros((8, LANES), F32)
        second = jnp.zeros((8, LANES), F32)
        for dr in range(-2 - r % 2, 4 - r % 2):
            for dc in (-2, -1, 0, 1, 2, 3):
                if max(abs(dr), abs(dc)) < 2:
                    continue
                s = source(r + dr + 2, dc)
                first = first + factor(same, dr, dc) * s
                second = second + factor(cross, dr, dc) * s
        store(r, (first + pltpu.roll(second, 64, 1))[0:cols])


def near_kernel(
    l3, l2, l1, top, bottom, west, east, diag,
    out3, out2, out1,
    r3, r2, r1, same, cross,
):
    for grid, region, (side, row_at, col_at) in zip((l3, l2, l1), (r3, r2, r1), LEVELS):
        for r in range(side):
            at = (r + 2) * PITCH + 4
            region[at : at + side, :] = grid[r * side : (r + 1) * side, :]
        for r in range(2):
            at = r * PITCH + 4
            region[at : at + side, :] = top[row_at + r * side : row_at + (r + 1) * side, :]
            at = (r + 2 + side) * PITCH + 4
            region[at : at + side, :] = bottom[row_at + r * side : row_at + (r + 1) * side, :]
        rows = side + 4
        for k in range(2):
            at = col_at + k * rows
            region[pl.ds(2 + k, rows, stride=PITCH), :] = west[at : at + rows, :]
            region[pl.ds(4 + side + k, rows, stride=PITCH), :] = east[at : at + rows, :]
    for level, region, side, out in ((4, r3, 8, out3), (3, r2, 4, out2), (2, r1, 2, out1)):
        def store(r, value, out=out):
            out[r] = value
        transfer_rows(
            region, diag.at[level], same.at[level - 2], cross.at[level - 2], side, side, store
        )


def near(l3, l2, l1, top, bottom, west, east, diag):
    shape = lambda *dims: jax.ShapeDtypeStruct(dims, F32)
    return pl.pallas_call(
        near_kernel,
        out_shape=(shape(8, 8, 128), shape(4, 4, 128), shape(2, 2, 128)),
        in_specs=[VMEM] * 8,
        out_specs=(VMEM,) * 3,
        scratch_shapes=[
            pltpu.VMEM((12 * PITCH, 128), F32),
            pltpu.VMEM((8 * PITCH, 128), F32),
            pltpu.VMEM((6 * PITCH, 128), F32),
            pltpu.VMEM((3, 56, 128), F32),
            pltpu.VMEM((3, 56, 128), F32),
        ],
        name="near",
    )(l3, l2, l1, top, bottom, west, east, diag)


def coarse_kernel(
    roots, shifts, diag,
    out0, outc, outt,
    grid, region, w_two, xc, xt, coarse, same, cross,
):
    wide_at = lax.axis_index("wide")
    narrow_at = lax.axis_index("narrow")
    grid[...] = jnp.zeros_like(grid)
    for r in range(16):
        at = (r + 3) * PITCH + 3
        grid[at : at + 8, :] = roots[r * 8 : (r + 1) * 8, :]
    for t in range(2):
        split_weights(shifts.at[t], w_two.at[t])

    gather_children(roots, xc, 8, 4)
    coarse[...] = merge(xc[...], w_two[1])
    gather_children(coarse, xt, 4, 2)
    top = merge(xt[...], w_two[0])
    for r in range(4):
        outt[r] = top[2 * r : 2 * r + 2]

    region[...] = jnp.zeros_like(region)
    for r in range(8):
        at = (r + 2) * PITCH + 4
        region[at : at + 4, :] = coarse[4 * r : 4 * r + 4, :]
    def store(r, value):
        outc[r] = value
    transfer_rows(region, diag.at[0], same.at[0], cross.at[0], 8, 4, store)

    make_factors(diag.at[1], same.at[1], cross.at[1])
    dc = lax.broadcasted_iota(jnp.int32, (8, LANES), 0) - 3
    col_ok = (dc >= -2 - narrow_at % 2) & (dc <= 3 - narrow_at % 2)
    far = (dc >= 2) | (dc <= -2)
    first = jnp.zeros((8, LANES), F32)
    second = jnp.zeros((8, LANES), F32)
    for dr in range(-3, 4):
        row_ok = (dr >= -2 - wide_at % 2) & (dr <= 3 - wide_at % 2)
        allowed = col_ok & row_ok
        if abs(dr) < 2:
            allowed = allowed & far
        s = grid[pl.ds((wide_at + dr + 3) * PITCH + narrow_at, 8), :]
        at = (dr + 3) * 7
        first = first + jnp.where(allowed, same[1, at : at + 8, :] * s, 0.0)
        second = second + jnp.where(allowed, cross[1, at : at + 8, :] * s, 0.0)
    total = first + pltpu.roll(second, 64, 1)
    out0[0] = jnp.sum(total, axis=0, keepdims=True)


def coarse_levels(roots, shifts, diag):
    shape = lambda *dims: jax.ShapeDtypeStruct(dims, F32)
    return pl.pallas_call(
        coarse_kernel,
        out_shape=(shape(1, 1, 128), shape(8, 4, 128), shape(4, 2, 128)),
        in_specs=[
            VMEM,
            pl.BlockSpec((2, 4, 128, 128), lambda i: (0, 0, 0, 0)),
            VMEM,
        ],
        out_specs=(VMEM,) * 3,
        grid=(1,),
        scratch_shapes=[
            pltpu.VMEM((22 * PITCH, 128), F32),
            pltpu.VMEM((12 * PITCH, 128), F32),
            pltpu.VMEM((2, 512, 256), BF16),
            pltpu.VMEM((32, 512), F32),
            pltpu.VMEM((8, 512), F32),
            pltpu.VMEM((32, 128), F32),
            pltpu.VMEM((2, 56, 128), F32),
            pltpu.VMEM((2, 56, 128), F32),
        ],
        name="coarse",
    )(roots, shifts, diag)


def shift_by(x, axis, step):
    count = lax.axis_size(axis)
    pairs = [(i, i + step) for i in range(count) if 0 <= i + step < count]
    return lax.ppermute(x, axis, pairs)


def local(offsets, strengths, leaf_map, shift_matrices, transfer_diagonal):
    leaf, l3, l2, l1, l0, up, down = upward(
        offsets.reshape(2, GROUPS, LANES),
        strengths.reshape(2, GROUPS, LANES),
        leaf_map.reshape(GROUPS, LANES),
        shift_matrices,
    )
    roots = lax.all_to_all(l0, ALL, 0, 0, tiled=True)
    top = shift_by(down, "wide", 1)
    bottom = shift_by(up, "wide", -1)
    to_west, to_east = pack(l3, l2, l1, top, bottom)
    west = shift_by(to_east, "narrow", 1)
    east = shift_by(to_west, "narrow", -1)
    local_three, local_two, local_one = near(l3, l2, l1, top, bottom, west, east, transfer_diagonal)
    local_zero, coarse_local, top_grid = coarse_levels(roots, shift_matrices, transfer_diagonal)
    return (
        leaf.reshape(32, 32, 128), local_zero, local_one, local_two, local_three,
        coarse_local, top_grid,
    )


def solution(mesh):
    return jax.shard_map(
        local,
        mesh=mesh,
        in_specs=(
            P(None, "wide", "narrow", None),
            P(None, "wide", "narrow", None),
            P("wide", "narrow", None),
            P(),
            P(),
        ),
        out_specs=(
            P("wide", "narrow", None),
            P("wide", "narrow", None),
            P("wide", "narrow", None),
            P("wide", "narrow", None),
            P("wide", "narrow", None),
            P(),
            P(),
        ),
        check_vma=False,
    )
```

time: 207 us -> 51.7 us (0.25)
  the two profiles are of different devices: /device:TPU:0 before, /device:TPU:7 now
where the time goes in v1:
time: 51.7 us; the launch traced here: 51.4 us
  starting transfers between devices  23.3 us (45%)
  Pallas kernels  17.2 us (33%)
  waiting for transfers between devices  8.37 us (16%)
  local copies, waits for them, and re-layouts  1.83 us (4%)
  between operations  0.72 us (1%)
    ppermute x4, starting transfers between devices, shift_by(): return lax.ppermute(x, axis, pairs)  12.5 us
    pallas_call x1, Pallas kernels, upward(): pl.pallas_call(up_kernel, out_shape=(shape(LEAVES, 128), shape(64, 128),...  11.6 us
    all_to_all x1, starting transfers between devices, local(): roots = lax.all_to_all(l0, ALL, 0, 0, tiled=True)  10.8 us
    ppermute x4, waiting for transfers between devices, shift_by(): return lax.ppermute(x, axis, pairs)  8.37 us
    pallas_call x1, Pallas kernels, coarse_levels(): pl.pallas_call(coarse_kernel, out_shape=(shape(1, 1, 128), shape(8, 4, 12...  2.13 us
    pallas_call x1, Pallas kernels, near(): pl.pallas_call(near_kernel, out_shape=(shape(8, 8, 128), shape(4, 4, 128)...  1.98 us
    unnamed x10, local copies, waits for them, and re-layouts  1.83 us
    pallas_call x1, Pallas kernels, pack(): pl.pallas_call(pack_kernel, out_shape=(jax.ShapeDtypeStruct((HALO_COLS, 1...  1.43 us
  transfers between devices with their start and end apart: 5, of which 2 were waited for; matrix products, arithmetic and copies ran while one was open for 0% of the time, Pallas kernels for 7%

profile of v1, /device:TPU:7, one launch (start us, length us, event | category | flops | bytes accessed | tf_op | source)
XLA Modules:
  0.0 51.4 jit_solution(13766770943917466667)
XLA Ops:
  0.6 11.6 %upward.1 = (f32[1024,128]{1,0:T(8,128)}, f32[64,128]{1,0:T(8,128)}, f32[16,128]{1,0:T(8,128)}, f32[8,128]{1,0:T(8,128)}, f32[128,128]{1,0:T(8,128)}, /*index=5*/f32[28,128]{1,0:T(8,128)}, f32[28,128]{1,0:T(8,128)}) custom-call(f32[2,64,128]{2,1,0:T(8,128)} %bitcast.9, f32[2,64,128]{2,1,0:T(8,128)} %bitcast.10, s32[64,128]{1,0:T(8,128)} %bitcast.12, ...), custom_call_target="tpu_custom_call" | custom-call | tf_op jit(solution)/shard_map/upward/pallas_call | solution.py:157
  12.3 10.8 %all-to-all-start = ((f32[128,1,128]{2,1,0:T(1,128)}), f32[128,1,128]{2,1,0:T(1,128)S(1)}, u32[]{:S(2)}, u32[]{:S(2)}) async-start(f32[128,1,128]{2,1,0:T(1,128)} %bitcast.11), calls=%async_computation | async-start | bytes 131072 | tf_op jit(solution)/shard_map/all_to_all | solution.py:385
  23.0 3.8 %collective-permute-start = (f32[28,128]{1,0:T(8,128)}, f32[28,128]{1,0:T(8,128)S(1)}, u32[]{:S(2)}, u32[]{:S(2)}) collective-permute-start(f32[28,128]{1,0:T(8,128)} %get-tuple-element.28), channel_id=1, source_target_pairs={{0,8},{8,16},{16,24},{24,32},{32,40},{40,48},{48,56},{56,64},{64,7... | collective-permute-start | bytes 43016 | tf_op jit(solution)/shard_map/ppermute | solution.py:375
  26.9 1.9 %collective-permute-start.1 = (f32[28,128]{1,0:T(8,128)}, f32[28,128]{1,0:T(8,128)S(1)}, u32[]{:S(2)}, u32[]{:S(2)}) collective-permute-start(f32[28,128]{1,0:T(8,128)} %get-tuple-element.29), channel_id=1, source_target_pairs={{8,0},{16,8},{24,16},{32,24},{40,32},{48,40},{56,48},{64,56},{72,6... | collective-permute-start | bytes 43016 | tf_op jit(solution)/shard_map/ppermute | solution.py:375
  28.8 0.0 collective-permute-done.top
  28.8 0.0 copy-start.1
  28.8 4.2 %collective-permute-done.1.bottom = f32[28,128]{1,0:T(8,128)S(1)} collective-permute-done((f32[28,128]{1,0:T(8,128)}, f32[28,128]{1,0:T(8,128)S(1)}, u32[]{:S(2)}, u32[]{:S(2)}) %collective-permute-start.1) | collective-permute-done | bytes 14368 | tf_op jit(solution)/shard_map/ppermute | solution.py:375
  33.0 0.0 copy-start.2
  33.0 0.0 copy-done.1
  33.0 0.6 %copy-done.2 = f32[28,128]{1,0:T(8,128)} copy-done((f32[28,128]{1,0:T(8,128)}, f32[28,128]{1,0:T(8,128)S(1)}, u32[]{:S(2)}) %copy-start.2) | copy-done | bytes 14360
  33.6 1.4 %pack.1 = (f32[52,128]{1,0:T(8,128)}, f32[52,128]{1,0:T(8,128)}) custom-call(f32[64,128]{1,0:T(8,128)} %get-tuple-element.25.l3, f32[16,128]{1,0:T(8,128)} %get-tuple-element.26.l2, f32[8,128]{1,0:T(8,128)} %get-tuple-element.27.l1, f32[28,128]{1,0:T(8,128)} %copy-done.1, f32[28,128]{1,0:T(8,128)} %copy-done.2), custom_call_target="tpu_custom_call" | custom-call | tf_op jit(solution)/shard_map/pack/pallas_call | solution.py:201
  35.1 3.7 %collective-permute-start.2 = (f32[52,128]{1,0:T(8,128)}, f32[52,128]{1,0:T(8,128)S(1)}, u32[]{:S(2)}, u32[]{:S(2)}) collective-permute-start(f32[52,128]{1,0:T(8,128)} %get-tuple-element.30), channel_id=1, source_target_pairs={{0,1},{1,2},{2,3},{3,4},{4,5},{5,6},{6,7},{8,9},{9,10},{10,11},{11... | collective-permute-start | bytes 79880 | tf_op jit(solution)/shard_map/ppermute | solution.py:375
  38.8 3.1 %collective-permute-start.3 = (f32[52,128]{1,0:T(8,128)}, f32[52,128]{1,0:T(8,128)S(1)}, u32[]{:S(2)}, u32[]{:S(2)}) collective-permute-start(f32[52,128]{1,0:T(8,128)} %get-tuple-element.31), channel_id=1, source_target_pairs={{1,0},{2,1},{3,2},{4,3},{5,4},{6,5},{7,6},{9,8},{10,9},{11,10},{12... | collective-permute-start | bytes 79880 | tf_op jit(solution)/shard_map/ppermute | solution.py:375
  41.9 0.0 collective-permute-done.2.west
  41.9 0.0 copy-start.3
  41.9 4.1 %collective-permute-done.3.east = f32[52,128]{1,0:T(8,128)S(1)} collective-permute-done((f32[52,128]{1,0:T(8,128)}, f32[52,128]{1,0:T(8,128)S(1)}, u32[]{:S(2)}, u32[]{:S(2)}) %collective-permute-start.3) | collective-permute-done | bytes 26656 | tf_op jit(solution)/shard_map/ppermute | solution.py:375
  46.0 0.0 copy-done.3
  46.0 0.0 copy-start.4
  46.0 0.6 %copy-done.4 = f32[52,128]{1,0:T(8,128)} copy-done((f32[52,128]{1,0:T(8,128)}, f32[52,128]{1,0:T(8,128)S(1)}, u32[]{:S(2)}) %copy-start.4) | copy-done | bytes 26648
  46.6 2.0 %near.1 = (f32[8,8,128]{2,1,0:T(8,128)}, f32[4,4,128]{2,1,0:T(4,128)}, f32[2,2,128]{2,1,0:T(2,128)}) custom-call(f32[64,128]{1,0:T(8,128)} %get-tuple-element.25.l3, f32[16,128]{1,0:T(8,128)} %get-tuple-element.26.l2, f32[8,128]{1,0:T(8,128)} %get-tuple-element.27.l1, f32[28,128]{1,0:T(8,128)} %copy-done.1, f32[28,128]{1,0:T(8,128)} %copy-done.2, ...), custom_call_target="tpu_custom_call" | custom-call | tf_op jit(solution)/shard_map/near/pallas_call | solution.py:282
  48.6 0.0 all-to-all-done
  48.6 0.0 copy-start
  48.6 0.6 %copy-done = f32[128,1,128]{2,1,0:T(1,128)} copy-done((f32[128,1,128]{2,1,0:T(1,128)}, f32[128,1,128]{2,1,0:T(1,128)S(1)}, u32[]{:S(2)}) %copy-start) | copy-done | bytes 65560
  49.2 2.1 %coarse.1 = (f32[1,1,128]{2,1,0:T(1,128)}, f32[8,4,128]{2,1,0:T(4,128)}, f32[4,2,128]{2,1,0:T(2,128)}) custom-call(f32[128,128]{1,0:T(8,128)} %bitcast.8, f32[7,4,128,128]{3,2,1,0:T(8,128)} %shifts.3, f32[5,49,128]{2,1,0:T(8,128)} %diag.3), custom_call_target="tpu_custom_call" | custom-call | tf_op jit(solution)/shard_map/coarse/pallas_call | solution.py:348
Async XLA Ops:
  12.3 36.3 %all-to-all-start = ((f32[128,1,128]{2,1,0:T(1,128)}), f32[128,1,128]{2,1,0:T(1,128)S(1)}, u32[]{:S(2)}, u32[]{:S(2)}) async-start(f32[128,1,128]{2,1,0:T(1,128)} %bitcast.11), calls=%async_computation | async-start | bytes 131072 | tf_op jit(solution)/shard_map/all_to_all | solution.py:385
  23.0 5.8 %collective-permute-start = (f32[28,128]{1,0:T(8,128)}, f32[28,128]{1,0:T(8,128)S(1)}, u32[]{:S(2)}, u32[]{:S(2)}) collective-permute-start(f32[28,128]{1,0:T(8,128)} %get-tuple-element.28), channel_id=1, source_target_pairs={{0,8},{8,16},{16,24},{24,32},{32,40},{40,48},{48,56},{56,64},{64,7... | collective-permute-start | bytes 43016 | tf_op jit(solution)/shard_map/ppermute | solution.py:375
  26.9 6.2 %collective-permute-start.1 = (f32[28,128]{1,0:T(8,128)}, f32[28,128]{1,0:T(8,128)S(1)}, u32[]{:S(2)}, u32[]{:S(2)}) collective-permute-start(f32[28,128]{1,0:T(8,128)} %get-tuple-element.29), channel_id=1, source_target_pairs={{8,0},{16,8},{24,16},{32,24},{40,32},{48,40},{56,48},{64,56},{72,6... | collective-permute-start | bytes 43016 | tf_op jit(solution)/shard_map/ppermute | solution.py:375
  28.8 4.2 %copy-start.1 = (f32[28,128]{1,0:T(8,128)}, f32[28,128]{1,0:T(8,128)S(1)}, u32[]{:S(2)}) copy-start(f32[28,128]{1,0:T(8,128)S(1)} %collective-permute-done.top) | copy-start | bytes 43012
  33.0 0.6 %copy-start.2 = (f32[28,128]{1,0:T(8,128)}, f32[28,128]{1,0:T(8,128)S(1)}, u32[]{:S(2)}) copy-start(f32[28,128]{1,0:T(8,128)S(1)} %collective-permute-done.1.bottom) | copy-start | bytes 43012
  35.1 6.8 %collective-permute-start.2 = (f32[52,128]{1,0:T(8,128)}, f32[52,128]{1,0:T(8,128)S(1)}, u32[]{:S(2)}, u32[]{:S(2)}) collective-permute-start(f32[52,128]{1,0:T(8,128)} %get-tuple-element.30), channel_id=1, source_target_pairs={{0,1},{1,2},{2,3},{3,4},{4,5},{5,6},{6,7},{8,9},{9,10},{10,11},{11... | collective-permute-start | bytes 79880 | tf_op jit(solution)/shard_map/ppermute | solution.py:375
  38.8 7.2 %collective-permute-start.3 = (f32[52,128]{1,0:T(8,128)}, f32[52,128]{1,0:T(8,128)S(1)}, u32[]{:S(2)}, u32[]{:S(2)}) collective-permute-start(f32[52,128]{1,0:T(8,128)} %get-tuple-element.31), channel_id=1, source_target_pairs={{1,0},{2,1},{3,2},{4,3},{5,4},{6,5},{7,6},{9,8},{10,9},{11,10},{12... | collective-permute-start | bytes 79880 | tf_op jit(solution)/shard_map/ppermute | solution.py:375
  41.9 4.2 %copy-start.3 = (f32[52,128]{1,0:T(8,128)}, f32[52,128]{1,0:T(8,128)S(1)}, u32[]{:S(2)}) copy-start(f32[52,128]{1,0:T(8,128)S(1)} %collective-permute-done.2.west) | copy-start | bytes 79876
  46.0 0.6 %copy-start.4 = (f32[52,128]{1,0:T(8,128)}, f32[52,128]{1,0:T(8,128)S(1)}, u32[]{:S(2)}) copy-start(f32[52,128]{1,0:T(8,128)S(1)} %collective-permute-done.3.east) | copy-start | bytes 79876
  48.6 0.6 %copy-start = (f32[128,1,128]{2,1,0:T(1,128)}, f32[128,1,128]{2,1,0:T(1,128)S(1)}, u32[]{:S(2)}) copy-start(f32[128,1,128]{2,1,0:T(1,128)S(1)} %all-to-all-done) | copy-start | bytes 196612

commit v2 on v1

v2 whole, which is shorter than its diff:
```python
import functools

import jax
import jax.numpy as jnp
from jax import lax
from jax.experimental import pallas as pl
from jax.experimental.pallas import tpu as pltpu
from jax.sharding import PartitionSpec as P

LANES = 128
GROUPS = 64
STEP = 16
LEAVES = 1024
ALL = ("wide", "narrow")
F32 = jnp.float32
BF16 = jnp.bfloat16
VMEM = pl.BlockSpec(memory_space=pltpu.VMEM)
ANY = pl.BlockSpec(memory_space=pl.ANY)
HALO_ROWS = 28
HALO_COLS = 52
CHUNK_WIDE = 32
CHUNK_NARROW = 72


def near_memory(*dims, kind=F32):
    return pltpu.VMEM(dims, kind)


def kept_near(*arrays):
    return tuple(pltpu.with_memory_space_constraint(a, pltpu.VMEM) for a in arrays)


PARTS = 4


def write_leaves(leaf, leaf_out, sem):
    rows = LEAVES // PARTS
    copies = [
        pltpu.make_async_copy(leaf.at[pl.ds(i * rows, rows)], leaf_out.at[pl.ds(i * rows, rows)], sem.at[i])
        for i in range(PARTS)
    ]
    for copy in copies:
        copy.start()
    return copies


def split_weights(src, dst):
    for quarter in range(4):
        rows = slice(quarter * 128, (quarter + 1) * 128)
        w = src[quarter]
        high = w.astype(BF16)
        dst[rows, 0:128] = high
        dst[rows, 128:256] = (w - high.astype(F32)).astype(BF16)


def merge(x, weights):
    count = x.shape[0]
    high = x.astype(BF16).astype(F32)
    both = jnp.concatenate([high, x - high], axis=0).astype(BF16)
    y = jnp.dot(both, weights, preferred_element_type=F32)
    return y[:count, :128] + y[:count, 128:] + y[count:, :128] + y[count:, 128:]


def gather_children(src, dst, rows, cols):
    for row_bit in range(2):
        for col_bit in range(2):
            quarter = 2 * row_bit + col_bit
            lanes = slice(quarter * 128, (quarter + 1) * 128)
            for r in range(rows):
                start = (2 * r + row_bit) * 2 * cols + col_bit
                if cols > 1:
                    piece = src[pl.ds(start, cols, stride=2), :]
                else:
                    piece = src[start : start + 1, :]
                dst[r * cols : (r + 1) * cols, lanes] = piece


def make_factors(diag, same, cross):
    lane = lax.broadcasted_iota(jnp.int32, (8, LANES), 1)
    for at in (0, 8, 16, 24, 32, 40, 41):
        rows = diag[at : at + 8, :]
        turned = pltpu.roll(rows, 64, 1)
        same[at : at + 8, :] = jnp.where(lane < 64, rows, turned)
        cross[at : at + 8, :] = jnp.where(lane < 64, turned, -rows)


def up_kernel(
    off, strg, lmap, diag, shifts,
    leaf, l3_out, l2_out, l1_out, send_out, w_low, same, cross,
    cheb, back, even, odd, acc, w_raw, w_two, x4, l4, x3, x2, x1, x0, w_sem,
):
    w_copy = pltpu.make_async_copy(shifts, w_raw, w_sem)
    w_copy.start()

    for i in range(2):
        a = off[i]
        t = [None] * 9
        t[0] = jnp.ones_like(a)
        t[1] = a
        t[2] = 2.0 * a * a - 1.0
        t[3] = 2.0 * t[2] * a - a
        t[4] = 2.0 * t[2] * t[2] - 1.0
        t[5] = 2.0 * t[3] * t[2] - a
        t[6] = 2.0 * t[3] * t[3] - 1.0
        t[7] = 2.0 * t[4] * t[3] - a
        t[8] = 2.0 * t[4] * t[4] - 1.0
        for j in range(9):
            cheb[i, j * GROUPS : (j + 1) * GROUPS, :] = t[j]
        for j in range(8):
            back[i, j * GROUPS : (j + 1) * GROUPS, :] = t[8 - j]

    def make_terms(g, out, j):
        blocks = []
        for i in range(2):
            now = cheb[i, pl.ds(g, 8, stride=GROUPS), :]
            before = back[i, pl.ds(g, 8, stride=GROUPS), :]
            twice = 2.0 * jnp.broadcast_to(cheb[i, pl.ds(8 * GROUPS + g, 1), :], (8, LANES))
            seq = [now]
            for _ in range(7):
                now, before = twice * now - before, now
                seq.append(now)
            blocks.append(seq)
        qr = jnp.broadcast_to(strg[0, pl.ds(g, 1), :], (8, LANES))
        qi = jnp.broadcast_to(strg[1, pl.ds(g, 1), :], (8, LANES))
        real = jnp.concatenate([qr * ca - qi * cb for ca, cb in zip(*blocks)], axis=0)
        imag = jnp.concatenate([qr * cb + qi * ca for ca, cb in zip(*blocks)], axis=0)
        whole = jnp.concatenate([real, imag], axis=0)
        high = whole.astype(BF16)
        lanes = slice(j * LANES, (j + 1) * LANES)
        out[0:128, lanes] = high
        out[128:256, lanes] = (whole - high.astype(F32)).astype(BF16)

    ids = lax.broadcasted_iota(jnp.int32, (256, LANES), 0).astype(F32).astype(BF16)
    one = jnp.ones((256, LANES), BF16)
    zero = jnp.zeros((256, LANES), BF16)

    def terms_of(k, out):
        for j in range(STEP):
            make_terms(k * STEP + j, out, j)

    def add_chunk(k, right):
        lefts = []
        for j in range(STEP):
            row = lmap[pl.ds(k * STEP + j, 1), :]
            parts = []
            for b in range(4):
                near = (row - 256 * b).astype(F32)
                near = jnp.broadcast_to(near, (256, LANES)).astype(BF16)
                parts.append(jnp.where(near == ids, one, zero))
            lefts.append(jnp.concatenate(parts, axis=0))
        left = jnp.concatenate(lefts, axis=1)
        return lax.dot_general(
            left, right[...], (((1,), (1,)), ((), ())), preferred_element_type=F32
        )

    terms_of(0, even)
    terms_of(1, odd)
    acc[...] = add_chunk(0, even)
    terms_of(2, even)
    acc[...] += add_chunk(1, odd)
    terms_of(3, odd)
    acc[...] += add_chunk(2, even)
    whole = acc[...] + add_chunk(3, odd)
    leaf[...] = whole[:, 0:128] + whole[:, 128:256]

    w_copy.wait()
    for t in range(2):
        split_weights(w_raw.at[t], w_low.at[t])
    for t in range(2, 7):
        split_weights(w_raw.at[t], w_two.at[t - 2])
    for level in range(5):
        make_factors(diag.at[level], same.at[level], cross.at[level])
    gather_children(leaf, x4, 16, 16)
    l4[...] = merge(x4[...], w_two[4])
    gather_children(l4, x3, 8, 8)
    l3_out[...] = merge(x3[...], w_two[3])
    gather_children(l3_out, x2, 4, 4)
    l2_out[...] = merge(x2[...], w_two[2])
    gather_children(l2_out, x1, 2, 2)
    l1_out[...] = merge(x1[...], w_two[1])
    gather_children(l1_out, x0, 1, 1)
    root = merge(x0[...], w_two[0])[0:1]
    send_out[pl.ds(HALO_ROWS, 16, stride=CHUNK_WIDE), :] = jnp.broadcast_to(root, (16, LANES))

    wide_at = lax.axis_index("wide")

    def put(chunk, l3_row, l2_row):
        at = pl.multiple_of(chunk * CHUNK_WIDE, 8)
        send_out[pl.ds(at, 16), :] = l3_out[l3_row : l3_row + 16, :]
        send_out[pl.ds(at + 16, 8), :] = l2_out[l2_row : l2_row + 8, :]
        send_out[pl.ds(at + 24, 4), :] = l1_out[0:4, :]

    @pl.when(wide_at > 0)
    def _():
        put(wide_at - 1, 0, 0)

    @pl.when(wide_at < 15)
    def _():
        put(wide_at + 1, 48, 8)


def upward(*operands):
    scratch = lambda dims, kind=F32: pltpu.VMEM(dims, kind)
    return pl.pallas_call(
        up_kernel,
        out_shape=(
            near_memory(LEAVES, 128), near_memory(64, 128), near_memory(16, 128),
            near_memory(8, 128), near_memory(16 * CHUNK_WIDE, 128),
            near_memory(2, 512, 256, kind=BF16), near_memory(5, 56, 128), near_memory(5, 56, 128),
        ),
        in_specs=[VMEM, VMEM, VMEM, VMEM, ANY],
        out_specs=(VMEM,) * 8,
        scratch_shapes=[
            scratch((2, 9 * GROUPS, LANES)),
            scratch((2, 8 * GROUPS, LANES)),
            scratch((256, STEP * LANES), BF16),
            scratch((256, STEP * LANES), BF16),
            scratch((LEAVES, 256)),
            scratch((7, 4, 128, 128)),
            scratch((5, 512, 256), BF16),
            scratch((256, 512)),
            scratch((256, 128)),
            scratch((64, 512)),
            scratch((16, 512)),
            scratch((8, 512)),
            scratch((8, 512)),
            pltpu.SemaphoreType.DMA,
        ],
        name="upward",
    )(*operands)


LEVELS = ((8, 0, 0), (4, 16, 24), (2, 24, 40))


def edge_rows(got, wide_at, top, bottom):
    above = pl.multiple_of(jnp.maximum(wide_at - 1, 0) * CHUNK_WIDE, 8)
    below = pl.multiple_of(jnp.minimum(wide_at + 1, 15) * CHUNK_WIDE, 8)
    top[...] = jnp.where(wide_at > 0, got[pl.ds(above, 32), :], 0.0)
    bottom[...] = jnp.where(wide_at < 15, got[pl.ds(below, 32), :], 0.0)


def pack_kernel(l3, l2, l1, got, send_out, top, bottom):
    wide_at = lax.axis_index("wide")
    narrow_at = lax.axis_index("narrow")
    edge_rows(got, wide_at, top, bottom)
    roots = got[pl.ds(HALO_ROWS, 16, stride=CHUNK_WIDE), :]
    for j in range(8):
        at = j * CHUNK_NARROW + HALO_COLS
        send_out[at : at + 16, :] = roots

    def put(chunk, first_of):
        base = pl.multiple_of(chunk * CHUNK_NARROW, 8)
        for grid, (side, row_at, col_at) in zip((l3, l2, l1), LEVELS):
            for k in range(2):
                at = base + col_at + k * (side + 4)
                c = first_of(side) + k
                send_out[pl.ds(at, 2), :] = top[pl.ds(row_at + c, 2, stride=side), :]
                send_out[pl.ds(at + 2, side), :] = grid[pl.ds(c, side, stride=side), :]
                send_out[pl.ds(at + 2 + side, 2), :] = bottom[pl.ds(row_at + c, 2, stride=side), :]

    @pl.when(narrow_at > 0)
    def _():
        put(narrow_at - 1, lambda side: 0)

    @pl.when(narrow_at < 7)
    def _():
        put(narrow_at + 1, lambda side: side - 2)


def pack(l3, l2, l1, got):
    return pl.pallas_call(
        pack_kernel,
        out_shape=(
            near_memory(8 * CHUNK_NARROW, 128), near_memory(32, 128), near_memory(32, 128),
        ),
        in_specs=[VMEM] * 4,
        out_specs=(VMEM,) * 3,
        name="pack",
    )(l3, l2, l1, got)


PITCH = 16


def transfer_rows(region, same, cross, side, cols, store):
    odd = (lax.broadcasted_iota(jnp.int32, (8, LANES), 0) % 2) == 1

    def factor(table, dr, dc):
        at = (dr + 3) * 7 + 3
        if dc < 3:
            return jnp.broadcast_to(table[at + dc : at + dc + 1, :], (8, LANES))
        right = jnp.broadcast_to(table[at + 3 : at + 4, :], (8, LANES))
        left = jnp.broadcast_to(table[at - 3 : at - 2, :], (8, LANES))
        return jnp.where(odd, left, right)

    def source(row, dc):
        base = row * PITCH + 4
        if dc < 3:
            return region[base + dc : base + dc + 8, :]
        return jnp.where(odd, region[base - 3 : base + 5, :], region[base + 3 : base + 11, :])

    for r in range(side):
        first = jnp.zeros((8, LANES), F32)
        second = jnp.zeros((8, LANES), F32)
        for dr in range(-2 - r % 2, 4 - r % 2):
            for dc in (-2, -1, 0, 1, 2, 3):
                if max(abs(dr), abs(dc)) < 2:
                    continue
                s = source(r + dr + 2, dc)
                first = first + factor(same, dr, dc) * s
                second = second + factor(cross, dr, dc) * s
        store(r, (first + pltpu.roll(second, 64, 1))[0:cols])


def down_kernel(
    l3, l2, l1, leaf, top, bottom, got_cols, w_two, same, cross,
    leaf_out, out0, out1, out2, out3, outc, outt,
    r3, r2, r1, west, east, grid, region, xc, xt, coarse, sem,
):
    copies = write_leaves(leaf, leaf_out, sem)
    wide_at = lax.axis_index("wide")
    narrow_at = lax.axis_index("narrow")
    before = pl.multiple_of(jnp.maximum(narrow_at - 1, 0) * CHUNK_NARROW, 8)
    after = pl.multiple_of(jnp.minimum(narrow_at + 1, 7) * CHUNK_NARROW, 8)
    west[...] = jnp.where(narrow_at > 0, got_cols[pl.ds(before, 56), :], 0.0)
    east[...] = jnp.where(narrow_at < 7, got_cols[pl.ds(after, 56), :], 0.0)

    grid[...] = jnp.zeros_like(grid)
    for j in range(8):
        at = j * CHUNK_NARROW + HALO_COLS
        grid[pl.ds(3 * PITCH + 3 + j, 16, stride=PITCH), :] = got_cols[at : at + 16, :]
    for row_bit in range(2):
        for col_bit in range(2):
            lanes = slice((2 * row_bit + col_bit) * 128, (2 * row_bit + col_bit + 1) * 128)
            for r in range(8):
                at = (2 * r + row_bit + 3) * PITCH + 3 + col_bit
                xc[4 * r : 4 * r + 4, lanes] = grid[pl.ds(at, 4, stride=2), :]
    coarse[...] = merge(xc[...], w_two[1])
    gather_children(coarse, xt, 4, 2)
    peak = merge(xt[...], w_two[0])
    for r in range(4):
        outt[r] = peak[2 * r : 2 * r + 2]

    for level, region_k, (side, row_at, col_at) in zip((l3, l2, l1), (r3, r2, r1), LEVELS):
        for r in range(side):
            at = (r + 2) * PITCH + 4
            region_k[at : at + side, :] = level[r * side : (r + 1) * side, :]
        for r in range(2):
            at = r * PITCH + 4
            region_k[at : at + side, :] = top[row_at + r * side : row_at + (r + 1) * side, :]
            at = (r + 2 + side) * PITCH + 4
            region_k[at : at + side, :] = bottom[row_at + r * side : row_at + (r + 1) * side, :]
        rows = side + 4
        for k in range(2):
            at = col_at + k * rows
            region_k[pl.ds(2 + k, rows, stride=PITCH), :] = west[at : at + rows, :]
            region_k[pl.ds(4 + side + k, rows, stride=PITCH), :] = east[at : at + rows, :]
    for level, region_k, side, out in ((4, r3, 8, out3), (3, r2, 4, out2), (2, r1, 2, out1)):
        def store(r, value, out=out):
            out[r] = value
        transfer_rows(region_k, same.at[level], cross.at[level], side, side, store)

    region[...] = jnp.zeros_like(region)
    for r in range(8):
        at = (r + 2) * PITCH + 4
        region[at : at + 4, :] = coarse[4 * r : 4 * r + 4, :]

    def store_coarse(r, value):
        outc[r] = value

    transfer_rows(region, same.at[0], cross.at[0], 8, 4, store_coarse)

    dc = lax.broadcasted_iota(jnp.int32, (8, LANES), 0) - 3
    col_ok = (dc >= -2 - narrow_at % 2) & (dc <= 3 - narrow_at % 2)
    far = (dc >= 2) | (dc <= -2)
    first = jnp.zeros((8, LANES), F32)
    second = jnp.zeros((8, LANES), F32)
    for dr in range(-3, 4):
        row_ok = (dr >= -2 - wide_at % 2) & (dr <= 3 - wide_at % 2)
        allowed = col_ok & row_ok
        if abs(dr) < 2:
            allowed = allowed & far
        s = grid[pl.ds((wide_at + dr + 3) * PITCH + narrow_at, 8), :]
        at = (dr + 3) * 7
        first = first + jnp.where(allowed, same[1, at : at + 8, :] * s, 0.0)
        second = second + jnp.where(allowed, cross[1, at : at + 8, :] * s, 0.0)
    total = first + pltpu.roll(second, 64, 1)
    out0[0] = jnp.sum(total, axis=0, keepdims=True)
    for copy in copies:
        copy.wait()


def downward(*operands):
    shape = lambda *dims: jax.ShapeDtypeStruct(dims, F32)
    tall = lambda rows: pltpu.VMEM((rows, 128), F32)
    return pl.pallas_call(
        down_kernel,
        out_shape=(
            shape(LEAVES, 128),
            shape(1, 1, 128), shape(2, 2, 128), shape(4, 4, 128), shape(8, 8, 128),
            shape(8, 4, 128), shape(4, 2, 128),
        ),
        in_specs=[VMEM] * 10,
        out_specs=(ANY,) + (VMEM,) * 6,
        scratch_shapes=[
            tall(12 * PITCH), tall(8 * PITCH), tall(6 * PITCH),
            tall(56), tall(56),
            tall(22 * PITCH), tall(12 * PITCH),
            pltpu.VMEM((32, 512), F32), pltpu.VMEM((8, 512), F32), tall(32),
            pltpu.SemaphoreType.DMA((PARTS,)),
        ],
        name="downward",
    )(*operands)


def local(offsets, strengths, leaf_map, shift_matrices, transfer_diagonal):
    leaf, l3, l2, l1, send, *tables = upward(
        offsets.reshape(2, GROUPS, LANES),
        strengths.reshape(2, GROUPS, LANES),
        leaf_map.reshape(GROUPS, LANES),
        transfer_diagonal,
        shift_matrices,
    )
    got_rows = lax.all_to_all(send, "wide", 0, 0, tiled=True)
    l3, l2, l1, got_rows = kept_near(l3, l2, l1, got_rows)
    send, top, bottom = pack(l3, l2, l1, got_rows)
    got_cols = lax.all_to_all(send, "narrow", 0, 0, tiled=True)
    leaf, local_zero, local_one, local_two, local_three, coarse_local, top_grid = downward(
        l3, l2, l1, *kept_near(leaf, top, bottom, got_cols, *tables)
    )
    return (
        leaf.reshape(32, 32, 128), local_zero, local_one, local_two, local_three,
        coarse_local, top_grid,
    )


def solution(mesh):
    return jax.shard_map(
        local,
        mesh=mesh,
        in_specs=(
            P(None, "wide", "narrow", None),
            P(None, "wide", "narrow", None),
            P("wide", "narrow", None),
            P(),
            P(),
        ),
        out_specs=(
            P("wide", "narrow", None),
            P("wide", "narrow", None),
            P("wide", "narrow", None),
            P("wide", "narrow", None),
            P("wide", "narrow", None),
            P(),
            P(),
        ),
        check_vma=False,
    )
```

time: 51.7 us -> 40.8 us (0.79)
  the two profiles are of different devices: /device:TPU:7 before, /device:TPU:0 now
where the time goes in v2:
time: 40.8 us; the launch traced here: 40.6 us
  blocking collectives  29.9 us (73%)
  Pallas kernels  10 us (25%)
  between operations  0.65 us (2%)
    all_to_all x1, blocking collectives, local(): got_cols = lax.all_to_all(send, 'narrow', 0, 0, tiled=True)  15.6 us
    all_to_all x1, blocking collectives, local(): got_rows = lax.all_to_all(send, 'wide', 0, 0, tiled=True)  14.3 us
    pallas_call x1, Pallas kernels, upward(): pl.pallas_call(up_kernel, out_shape=(near_memory(LEAVES, 128), near_memor...  8.07 us
    pallas_call x1, Pallas kernels, downward(): pl.pallas_call(down_kernel, out_shape=(shape(LEAVES, 128), shape(1, 1, 12...  1.93 us

profile of v2, /device:TPU:0, one launch (start us, length us, event | category | flops | bytes accessed | tf_op | source)
XLA Modules:
  0.0 40.6 jit_solution(13925409193192208713)
XLA Ops:
  0.6 8.1 %upward.1 = (f32[1024,128]{1,0:T(8,128)S(1)}, f32[64,128]{1,0:T(8,128)S(1)}, f32[16,128]{1,0:T(8,128)S(1)}, f32[8,128]{1,0:T(8,128)S(1)}, f32[512,128]{1,0:T(8,1...) custom-call(f32[2,64,128]{2,1,0:T(8,128)} %bitcast.12, ...), custom_call_target="tpu_custom_call" | custom-call | tf_op jit(solution)/shard_map/upward/pallas_call | solution.py:204
  8.7 14.3 %all_to_all.22 = f32[16,32,128]{2,1,0:T(8,128)S(1)} all-to-all(f32[16,32,128]{2,1,0:T(8,128)S(1)} %bitcast.11), channel_id=1, replica_groups=mesh['wide'=16,'narrow'=8] {'wide'}, dimensions={0} | all-to-all | bytes 524288 | tf_op jit(solution)/shard_map/all_to_all | solution.py:425
  23.0 15.6 %all_to_all.23 = f32[8,72,128]{2,1,0:T(8,128)S(1)} all-to-all(f32[8,72,128]{2,1,0:T(8,128)S(1)} %bitcast.10), channel_id=1, replica_groups=mesh['wide'=16,'narrow'=8] {'narrow'}, dimensions={0} | all-to-all | bytes 589824 | tf_op jit(solution)/shard_map/all_to_all | solution.py:428
  38.6 1.9 %downward.1 = (f32[1024,128]{1,0:T(8,128)}, f32[1,1,128]{2,1,0:T(1,128)}, f32[2,2,128]{2,1,0:T(2,128)}, f32[4,4,128]{2,1,0:T(4,128)}, f32[8,8,128]{2,1,0:T(8,128...) custom-call(f32[64,128]{1,0:T(8,128)S(1)} %get-tuple-element.25.l3, f32[16,128]{1,0:T(8,128)S(1)} %get-tuple-element.26.l2, ...), custom_call_target="tpu_custom_call" | custom-call | tf_op jit(solution)/shard_map/downward/pallas_call | solution.py:397
  (1 shorter events, 0.0 us)

commit v3 on v2

--- a/solution.py
+++ b/solution.py
@@ -9,7 +9,7 @@
 
 LANES = 128
 GROUPS = 64
-STEP = 16
+CHUNKS = (16, 16, 16, 16)
 LEAVES = 1024
 ALL = ("wide", "narrow")
 F32 = jnp.float32
@@ -17,9 +17,8 @@
 VMEM = pl.BlockSpec(memory_space=pltpu.VMEM)
 ANY = pl.BlockSpec(memory_space=pl.ANY)
 HALO_ROWS = 28
-HALO_COLS = 52
-CHUNK_WIDE = 32
-CHUNK_NARROW = 72
+CHUNK_WIDE = 29
+CHUNK_NARROW = 44
 
 
 def near_memory(*dims, kind=F32):
@@ -86,8 +85,8 @@
 
 def up_kernel(
     off, strg, lmap, diag, shifts,
-    leaf, l3_out, l2_out, l1_out, send_out, w_low, same, cross,
-    cheb, back, even, odd, acc, w_raw, w_two, x4, l4, x3, x2, x1, x0, w_sem,
+    leaf_out, l3_out, l2_out, l1_out, send_out, w_low, same, cross,
+    cheb, back, even, odd, acc, leaf, w_raw, w_two, x4, l4, x3, x2, x1, x0, w_sem, o_sem,
 ):
     w_copy = pltpu.make_async_copy(shifts, w_raw, w_sem)
     w_copy.start()
@@ -134,14 +133,14 @@
     one = jnp.ones((256, LANES), BF16)
     zero = jnp.zeros((256, LANES), BF16)
 
-    def terms_of(k, out):
-        for j in range(STEP):
-            make_terms(k * STEP + j, out, j)
-
-    def add_chunk(k, right):
+    def terms_of(groups, out):
+        for j, g in enumerate(groups):
+            make_terms(g, out, j)
+
+    def sums_of(groups, right):
         lefts = []
-        for j in range(STEP):
-            row = lmap[pl.ds(k * STEP + j, 1), :]
+        for g in groups:
+            row = lmap[pl.ds(g, 1), :]
             parts = []
             for b in range(4):
                 near = (row - 256 * b).astype(F32)
@@ -150,26 +149,34 @@
             lefts.append(jnp.concatenate(parts, axis=0))
         left = jnp.concatenate(lefts, axis=1)
         return lax.dot_general(
-            left, right[...], (((1,), (1,)), ((), ())), preferred_element_type=F32
+            left, right[:, 0 : len(groups) * LANES], (((1,), (1,)), ((), ())),
+            preferred_element_type=F32,
         )
 
-    terms_of(0, even)
-    terms_of(1, odd)
-    acc[...] = add_chunk(0, even)
-    terms_of(2, even)
-    acc[...] += add_chunk(1, odd)
-    terms_of(3, odd)
-    acc[...] += add_chunk(2, even)
-    whole = acc[...] + add_chunk(3, odd)
-    leaf[...] = whole[:, 0:128] + whole[:, 128:256]
-
-    w_copy.wait()
-    for t in range(2):
-        split_weights(w_raw.at[t], w_low.at[t])
-    for t in range(2, 7):
-        split_weights(w_raw.at[t], w_two.at[t - 2])
+    chunks, at = [], 0
+    for size in CHUNKS:
+        chunks.append(range(at, at + size))
+        at += size
+    buffers = (even, odd)
+    terms_of(chunks[0], even)
     for level in range(5):
         make_factors(diag.at[level], same.at[level], cross.at[level])
+    for k, groups in enumerate(chunks):
+        if k + 1 < len(chunks):
+            terms_of(chunks[k + 1], buffers[(k + 1) % 2])
+        part = sums_of(groups, buffers[k % 2])
+        if k == 0:
+            acc[...] = part
+        elif k + 1 < len(chunks):
+            acc[...] += part
+        else:
+            part = acc[...] + part
+            leaf[...] = part[:, 0:128] + part[:, 128:256]
+    copies = write_leaves(leaf, leaf_out, o_sem)
+    w_copy.wait()
+    for t in range(7):
+        split_weights(w_raw.at[t], w_low.at[t] if t < 2 else w_two.at[t - 2])
+
     gather_children(leaf, x4, 16, 16)
     l4[...] = merge(x4[...], w_two[4])
     gather_children(l4, x3, 8, 8)
@@ -185,7 +192,7 @@
     wide_at = lax.axis_index("wide")
 
     def put(chunk, l3_row, l2_row):
-        at = pl.multiple_of(chunk * CHUNK_WIDE, 8)
+        at = chunk * CHUNK_WIDE
         send_out[pl.ds(at, 16), :] = l3_out[l3_row : l3_row + 16, :]
         send_out[pl.ds(at + 16, 8), :] = l2_out[l2_row : l2_row + 8, :]
         send_out[pl.ds(at + 24, 4), :] = l1_out[0:4, :]
@@ -197,6 +204,9 @@
     @pl.when(wide_at < 15)
     def _():
         put(wide_at + 1, 48, 8)
+
+    for copy in copies:
+        copy.wait()
 
 
 def upward(*operands):
@@ -204,18 +214,19 @@
     return pl.pallas_call(
         up_kernel,
         out_shape=(
-            near_memory(LEAVES, 128), near_memory(64, 128), near_memory(16, 128),
+            jax.ShapeDtypeStruct((LEAVES, 128), F32), near_memory(64, 128), near_memory(16, 128),
             near_memory(8, 128), near_memory(16 * CHUNK_WIDE, 128),
             near_memory(2, 512, 256, kind=BF16), near_memory(5, 56, 128), near_memory(5, 56, 128),
         ),
         in_specs=[VMEM, VMEM, VMEM, VMEM, ANY],
-        out_specs=(VMEM,) * 8,
+        out_specs=(ANY,) + (VMEM,) * 7,
         scratch_shapes=[
             scratch((2, 9 * GROUPS, LANES)),
             scratch((2, 8 * GROUPS, LANES)),
-            scratch((256, STEP * LANES), BF16),
-            scratch((256, STEP * LANES), BF16),
+            scratch((256, max(CHUNKS) * LANES), BF16),
+            scratch((256, max(CHUNKS) * LANES), BF16),
             scratch((LEAVES, 256)),
+            scratch((LEAVES, 128)),
             scratch((7, 4, 128, 128)),
             scratch((5, 512, 256), BF16),
             scratch((256, 512)),
@@ -225,62 +236,15 @@
             scratch((8, 512)),
             scratch((8, 512)),
             pltpu.SemaphoreType.DMA,
+            pltpu.SemaphoreType.DMA((PARTS,)),
         ],
         name="upward",
     )(*operands)
 
 
-LEVELS = ((8, 0, 0), (4, 16, 24), (2, 24, 40))
-
-
-def edge_rows(got, wide_at, top, bottom):
-    above = pl.multiple_of(jnp.maximum(wide_at - 1, 0) * CHUNK_WIDE, 8)
-    below = pl.multiple_of(jnp.minimum(wide_at + 1, 15) * CHUNK_WIDE, 8)
-    top[...] = jnp.where(wide_at > 0, got[pl.ds(above, 32), :], 0.0)
-    bottom[...] = jnp.where(wide_at < 15, got[pl.ds(below, 32), :], 0.0)
-
-
-def pack_kernel(l3, l2, l1, got, send_out, top, bottom):
-    wide_at = lax.axis_index("wide")
-    narrow_at = lax.axis_index("narrow")
-    edge_rows(got, wide_at, top, bottom)
-    roots = got[pl.ds(HALO_ROWS, 16, stride=CHUNK_WIDE), :]
-    for j in range(8):
-        at = j * CHUNK_NARROW + HALO_COLS
-        send_out[at : at + 16, :] = roots
-
-    def put(chunk, first_of):
-        base = pl.multiple_of(chunk * CHUNK_NARROW, 8)
-        for grid, (side, row_at, col_at) in zip((l3, l2, l1), LEVELS):
-            for k in range(2):
-                at = base + col_at + k * (side + 4)
-                c = first_of(side) + k
-                send_out[pl.ds(at, 2), :] = top[pl.ds(row_at + c, 2, stride=side), :]
-                send_out[pl.ds(at + 2, side), :] = grid[pl.ds(c, side, stride=side), :]
-                send_out[pl.ds(at + 2 + side, 2), :] = bottom[pl.ds(row_at + c, 2, stride=side), :]
-
-    @pl.when(narrow_at > 0)
-    def _():
-        put(narrow_at - 1, lambda side: 0)
-
-    @pl.when(narrow_at < 7)
-    def _():
-        put(narrow_at + 1, lambda side: side - 2)
-
-
-def pack(l3, l2, l1, got):
-    return pl.pallas_call(
-        pack_kernel,
-        out_shape=(
-            near_memory(8 * CHUNK_NARROW, 128), near_memory(32, 128), near_memory(32, 128),
-        ),
-        in_specs=[VMEM] * 4,
-        out_specs=(VMEM,) * 3,
-        name="pack",
-    )(l3, l2, l1, got)
-
-
 PITCH = 16
+LEVELS = ((8, 0), (4, 16), (2, 24))
+SAVED = (0, 64, 96)
 
 
 def transfer_rows(region, same, cross, side, cols, store):
@@ -313,23 +277,93 @@
         store(r, (first + pltpu.roll(second, 64, 1))[0:cols])
 
 
-def down_kernel(
-    l3, l2, l1, leaf, top, bottom, got_cols, w_two, same, cross,
-    leaf_out, out0, out1, out2, out3, outc, outt,
-    r3, r2, r1, west, east, grid, region, xc, xt, coarse, sem,
-):
-    copies = write_leaves(leaf, leaf_out, sem)
+def column_products(column, same, cross, dcs):
+    odd = (lax.broadcasted_iota(jnp.int32, (8, LANES), 0) % 2) == 1
+    first = jnp.zeros((8, LANES), F32)
+    second = jnp.zeros((8, LANES), F32)
+
+    def factor(table, dr, dc):
+        at = (dr + 3) * 7 + dc + 3
+        if dr < 3:
+            return jnp.broadcast_to(table[at : at + 1, :], (8, LANES))
+        low = jnp.broadcast_to(table[dc + 3 : dc + 4, :], (8, LANES))
+        high = jnp.broadcast_to(table[at : at + 1, :], (8, LANES))
+        return jnp.where(odd, low, high)
+
+    for k, dc in enumerate(dcs):
+        for dr in (-2, -1, 0, 1, 2, 3):
+            if max(abs(dr), abs(dc)) < 2:
+                continue
+            at = k * PITCH + 4
+            if dr < 3:
+                s = column[at + dr : at + dr + 8, :]
+            else:
+                s = jnp.where(odd, column[at - 3 : at + 5, :], column[at + 3 : at + 11, :])
+            first = first + factor(same, dr, dc) * s
+            second = second + factor(cross, dr, dc) * s
+    return first + pltpu.roll(second, 64, 1)
+
+
+def pack_kernel(l3, l2, l1, got, same, cross, send_out, top, bottom, columns):
     wide_at = lax.axis_index("wide")
     narrow_at = lax.axis_index("narrow")
-    before = pl.multiple_of(jnp.maximum(narrow_at - 1, 0) * CHUNK_NARROW, 8)
-    after = pl.multiple_of(jnp.minimum(narrow_at + 1, 7) * CHUNK_NARROW, 8)
-    west[...] = jnp.where(narrow_at > 0, got_cols[pl.ds(before, 56), :], 0.0)
-    east[...] = jnp.where(narrow_at < 7, got_cols[pl.ds(after, 56), :], 0.0)
-
+    above = jnp.maximum(wide_at - 1, 0) * CHUNK_WIDE
+    below = jnp.minimum(wide_at + 1, 15) * CHUNK_WIDE
+    top[0:HALO_ROWS, :] = jnp.where(wide_at > 0, got[pl.ds(above, HALO_ROWS), :], 0.0)
+    bottom[0:HALO_ROWS, :] = jnp.where(wide_at < 15, got[pl.ds(below, HALO_ROWS), :], 0.0)
+    roots = got[pl.ds(HALO_ROWS, 16, stride=CHUNK_WIDE), :]
+    for j in range(8):
+        at = j * CHUNK_NARROW + HALO_ROWS
+        send_out[at : at + 16, :] = roots
+
+    results = []
+    for number, (grid, (side, row_at)) in enumerate(zip((l3, l2, l1), LEVELS)):
+        level = 4 - number
+        for east in range(2):
+            column = columns.at[2 * number + east]
+            for k in range(2):
+                c = k + east * (side - 2)
+                at = k * PITCH + 2
+                column[at : at + 2, :] = top[pl.ds(row_at + c, 2, stride=side), :]
+                column[at + 2 : at + 2 + side, :] = grid[pl.ds(c, side, stride=side), :]
+                column[at + 2 + side : at + 4 + side, :] = bottom[pl.ds(row_at + c, 2, stride=side), :]
+            for target, dcs in enumerate(((-2, -1), (-3, -2)) if east else ((2, 3), (1, 2))):
+                value = column_products(column, same.at[level], cross.at[level], dcs)
+                results.append((east, row_at + target * side, value[0:side]))
+
+    for east in range(2):
+        @pl.when((narrow_at < 7) if east else (narrow_at > 0))
+        def _():
+            base = (narrow_at + (1 if east else -1)) * CHUNK_NARROW
+            for which, at, value in results:
+                if which == east:
+                    send_out[pl.ds(base + at, value.shape[0]), :] = value
+
+
+def pack(*operands):
+    return pl.pallas_call(
+        pack_kernel,
+        out_shape=(
+            near_memory(8 * CHUNK_NARROW, 128), near_memory(32, 128), near_memory(32, 128),
+        ),
+        in_specs=[VMEM] * 6,
+        out_specs=(VMEM,) * 3,
+        scratch_shapes=[pltpu.VMEM((6, 2 * PITCH, 128), F32)],
+        name="pack",
+    )(*operands)
+
+
+def down_kernel(
+    l3, l2, l1, top, bottom, got, w_two, same, cross,
+    out0, out1, out2, out3, outc, outt,
+    r3, r2, r1, total, grid, region, xc, xt, coarse,
+):
+    wide_at = lax.axis_index("wide")
+    narrow_at = lax.axis_index("narrow")
     grid[...] = jnp.zeros_like(grid)
     for j in range(8):
-        at = j * CHUNK_NARROW + HALO_COLS
-        grid[pl.ds(3 * PITCH + 3 + j, 16, stride=PITCH), :] = got_cols[at : at + 16, :]
+        at = j * CHUNK_NARROW + HALO_ROWS
+        grid[pl.ds(3 * PITCH + 3 + j, 16, stride=PITCH), :] = got[at : at + 16, :]
     for row_bit in range(2):
         for col_bit in range(2):
             lanes = slice((2 * row_bit + col_bit) * 128, (2 * row_bit + col_bit + 1) * 128)
@@ -342,24 +376,36 @@
     for r in range(4):
         outt[r] = peak[2 * r : 2 * r + 2]
 
-    for level, region_k, (side, row_at, col_at) in zip((l3, l2, l1), (r3, r2, r1), LEVELS):
+    for number, (own, region_k, (side, row_at)) in enumerate(
+        zip((l3, l2, l1), (r3, r2, r1), LEVELS)
+    ):
+        region_k[...] = jnp.zeros_like(region_k)
         for r in range(side):
             at = (r + 2) * PITCH + 4
-            region_k[at : at + side, :] = level[r * side : (r + 1) * side, :]
+            region_k[at : at + side, :] = own[r * side : (r + 1) * side, :]
         for r in range(2):
             at = r * PITCH + 4
             region_k[at : at + side, :] = top[row_at + r * side : row_at + (r + 1) * side, :]
             at = (r + 2 + side) * PITCH + 4
             region_k[at : at + side, :] = bottom[row_at + r * side : row_at + (r + 1) * side, :]
-        rows = side + 4
-        for k in range(2):
-            at = col_at + k * rows
-            region_k[pl.ds(2 + k, rows, stride=PITCH), :] = west[at : at + rows, :]
-            region_k[pl.ds(4 + side + k, rows, stride=PITCH), :] = east[at : at + rows, :]
-    for level, region_k, side, out in ((4, r3, 8, out3), (3, r2, 4, out2), (2, r1, 2, out1)):
-        def store(r, value, out=out):
-            out[r] = value
-        transfer_rows(region_k, same.at[level], cross.at[level], side, side, store)
+
+        def store(r, value, base=SAVED[number]):
+            total[base + 8 * r : base + 8 * r + 8, :] = value
+
+        level = 4 - number
+        transfer_rows(region_k, same.at[level], cross.at[level], side, 8, store)
+    before = jnp.maximum(narrow_at - 1, 0) * CHUNK_NARROW
+    after = jnp.minimum(narrow_at + 1, 7) * CHUNK_NARROW
+    for number, (side, at) in enumerate(LEVELS):
+        for start, there, first in ((before, narrow_at > 0, 0), (after, narrow_at < 7, side - 2)):
+            for k in range(2):
+                given = jnp.where(there, got[pl.ds(start + at + k * side, side), :], 0.0)
+                rows = pl.ds(SAVED[number] + first + k, side, stride=8)
+                total[rows, :] = total[rows, :] + given
+    for number, ((side, _), out) in enumerate(zip(LEVELS, (out3, out2, out1))):
+        for r in range(side):
+            at = SAVED[number] + 8 * r
+            out[r] = total[at : at + side, :]
 
     region[...] = jnp.zeros_like(region)
     for r in range(8):
@@ -385,10 +431,8 @@
         at = (dr + 3) * 7
         first = first + jnp.where(allowed, same[1, at : at + 8, :] * s, 0.0)
         second = second + jnp.where(allowed, cross[1, at : at + 8, :] * s, 0.0)
-    total = first + pltpu.roll(second, 64, 1)
-    out0[0] = jnp.sum(total, axis=0, keepdims=True)
-    for copy in copies:
-        copy.wait()
+    own = first + pltpu.roll(second, 64, 1)
+    out0[0] = jnp.sum(own, axis=0, keepdims=True)
 
 
 def downward(*operands):
@@ -397,37 +441,38 @@
     return pl.pallas_call(
         down_kernel,
         out_shape=(
-            shape(LEAVES, 128),
             shape(1, 1, 128), shape(2, 2, 128), shape(4, 4, 128), shape(8, 8, 128),
             shape(8, 4, 128), shape(4, 2, 128),
         ),
-        in_specs=[VMEM] * 10,
-        out_specs=(ANY,) + (VMEM,) * 6,
+        in_specs=[VMEM] * 9,
+        out_specs=(VMEM,) * 6,
         scratch_shapes=[
-            tall(12 * PITCH), tall(8 * PITCH), tall(6 * PITCH),
-            tall(56), tall(56),
-            tall(22 * PITCH), tall(12 * PITCH),
+            tall(12 * PITCH), tall(8 * PITCH), tall(6 * PITCH), tall(112), tall(22 * PITCH), tall(12 * PITCH),
             pltpu.VMEM((32, 512), F32), pltpu.VMEM((8, 512), F32), tall(32),
-            pltpu.SemaphoreType.DMA((PARTS,)),
         ],
         name="downward",
     )(*operands)
 
 
+def exchange(boxes, axis):
+    return lax.all_to_all(boxes[:, None, :], axis, 0, 0, tiled=True)[:, 0, :]
+
+
 def local(offsets, strengths, leaf_map, shift_matrices, transfer_diagonal):
-    leaf, l3, l2, l1, send, *tables = upward(
+    leaf, l3, l2, l1, send, w_two, same, cross = upward(
         offsets.reshape(2, GROUPS, LANES),
         strengths.reshape(2, GROUPS, LANES),
         leaf_map.reshape(GROUPS, LANES),
         transfer_diagonal,
         shift_matrices,
     )
-    got_rows = lax.all_to_all(send, "wide", 0, 0, tiled=True)
-    l3, l2, l1, got_rows = kept_near(l3, l2, l1, got_rows)
-    send, top, bottom = pack(l3, l2, l1, got_rows)
-    got_cols = lax.all_to_all(send, "narrow", 0, 0, tiled=True)
-    leaf, local_zero, local_one, local_two, local_three, coarse_local, top_grid = downward(
-        l3, l2, l1, *kept_near(leaf, top, bottom, got_cols, *tables)
+    l3, l2, l1, got, w_two, same, cross = kept_near(
+        l3, l2, l1, exchange(send, "wide"), w_two, same, cross
+    )
+    send, top, bottom = pack(l3, l2, l1, got, same, cross)
+    top, bottom, got = kept_near(top, bottom, exchange(send, "narrow"))
+    local_zero, local_one, local_two, local_three, coarse_local, top_grid = downward(
+        l3, l2, l1, top, bottom, got, w_two, same, cross
     )
     return (
         leaf.reshape(32, 32, 128), local_zero, local_one, local_two, local_three,

time: 40.8 us -> 39.3 us (0.963)
  blocking collectives: 29.9 us -> 28.8 us
  Pallas kernels: 10 us -> 9.57 us
    all_to_all x2, blocking collectives: 29.9 us -> 28.8 us  [exchange(): return lax.all_to_all(boxes[:, None, :], axis, 0, 0, tiled=True)[:, 0, :]]
    pallas_call x2, Pallas kernels: 10 us -> 9.4 us  [the longest x1 8.11 us: upward(): pl.pallas_call(up_kernel, out_shape=(jax.ShapeDtypeStruct((LEAVES, 128),...]
where the time goes in v3:
time: 39.3 us; the launch traced here: 39.1 us
  blocking collectives  28.8 us (73%)
  Pallas kernels  9.57 us (24%)
  between operations  0.64 us (2%)
    all_to_all x2, blocking collectives, exchange(): return lax.all_to_all(boxes[:, None, :], axis, 0, 0, tiled=True)[:, 0, :]  28.8 us
    pallas_call x1, Pallas kernels, upward(): pl.pallas_call(up_kernel, out_shape=(jax.ShapeDtypeStruct((LEAVES, 128),...  8.11 us
    pallas_call x1, Pallas kernels, downward(): pl.pallas_call(down_kernel, out_shape=(shape(1, 1, 128), shape(2, 2, 128)...  1.3 us

profile of v3, /device:TPU:0, one launch (start us, length us, event | category | flops | bytes accessed | tf_op | source)
XLA Modules:
  0.0 39.1 jit_solution(15309865507581489861)
XLA Ops:
  0.6 8.1 %upward.1 = (f32[1024,128]{1,0:T(8,128)}, f32[64,128]{1,0:T(8,128)S(1)}, f32[16,128]{1,0:T(8,128)S(1)}, f32[8,128]{1,0:T(8,128)S(1)}, f32[464,128]{1,0:T(8,128)S...) custom-call(f32[2,64,128]{2,1,0:T(8,128)} %bitcast.16, ...), custom_call_target="tpu_custom_call" | custom-call | tf_op jit(solution)/shard_map/upward/pallas_call | solution.py:214
  8.7 14.0 %all_to_all.10 = f32[464,1,128]{2,1,0:T(1,128)S(1)} all-to-all(f32[464,1,128]{2,1,0:T(1,128)S(1)} %bitcast.14), channel_id=1, replica_groups=mesh['wide'=16,'narrow'=8] {'wide'}, dimensions={0} | all-to-all | bytes 475136 | tf_op jit(solution)/shard_map/all_to_all | solution.py:458
  22.8 0.2 pack.1
  22.9 14.8 %all_to_all.11 = f32[352,1,128]{2,1,0:T(1,128)S(1)} all-to-all(f32[352,1,128]{2,1,0:T(1,128)S(1)} %bitcast.15), channel_id=1, replica_groups=mesh['wide'=16,'narrow'=8] {'narrow'}, dimensions={0} | all-to-all | bytes 360448 | tf_op jit(solution)/shard_map/all_to_all | solution.py:458
  37.8 1.3 %downward.1 = (f32[1,1,128]{2,1,0:T(1,128)}, f32[2,2,128]{2,1,0:T(2,128)}, f32[4,4,128]{2,1,0:T(4,128)}, f32[8,8,128]{2,1,0:T(8,128)}, f32[8,4,128]{2,1,0:T(4,128)}, /*index=5*/f32[4,2,128]{2,1,0:T(2,128)}) custom-call(f32[64,128]{1,0:T(8,128)S(1)} %get-tuple-element.25.l3, f32[16,128]{1,0:T(8,128)S(1)} %get-tuple-element.26.l2, ...), custom_call_target="tpu_custom_call" | custom-call | tf_op jit(solution)/shard_map/downward/pallas_call | solution.py:441

commit v4 on v3

--- a/solution.py
+++ b/solution.py
@@ -1,11 +1,10 @@
-import functools
-
 import jax
 import jax.numpy as jnp
 from jax import lax
 from jax.experimental import pallas as pl
 from jax.experimental.pallas import tpu as pltpu
 from jax.sharding import PartitionSpec as P
+
 
 LANES = 128
 GROUPS = 64
@@ -17,8 +16,6 @@
 VMEM = pl.BlockSpec(memory_space=pltpu.VMEM)
 ANY = pl.BlockSpec(memory_space=pl.ANY)
 HALO_ROWS = 28
-CHUNK_WIDE = 29
-CHUNK_NARROW = 44
 
 
 def near_memory(*dims, kind=F32):
@@ -85,7 +82,7 @@
 
 def up_kernel(
     off, strg, lmap, diag, shifts,
-    leaf_out, l3_out, l2_out, l1_out, send_out, w_low, same, cross,
+    leaf_out, l3_out, l2_out, l1_out, even_out, odd_out, l0_out, w_low, same, cross,
     cheb, back, even, odd, acc, leaf, w_raw, w_two, x4, l4, x3, x2, x1, x0, w_sem, o_sem,
 ):
     w_copy = pltpu.make_async_copy(shifts, w_raw, w_sem)
@@ -187,23 +184,15 @@
     l1_out[...] = merge(x1[...], w_two[1])
     gather_children(l1_out, x0, 1, 1)
     root = merge(x0[...], w_two[0])[0:1]
-    send_out[pl.ds(HALO_ROWS, 16, stride=CHUNK_WIDE), :] = jnp.broadcast_to(root, (16, LANES))
-
-    wide_at = lax.axis_index("wide")
-
-    def put(chunk, l3_row, l2_row):
-        at = chunk * CHUNK_WIDE
-        send_out[pl.ds(at, 16), :] = l3_out[l3_row : l3_row + 16, :]
-        send_out[pl.ds(at + 16, 8), :] = l2_out[l2_row : l2_row + 8, :]
-        send_out[pl.ds(at + 24, 4), :] = l1_out[0:4, :]
-
-    @pl.when(wide_at > 0)
-    def _():
-        put(wide_at - 1, 0, 0)
-
-    @pl.when(wide_at < 15)
-    def _():
-        put(wide_at + 1, 48, 8)
+    l0_out[...] = jnp.broadcast_to(root, (128, LANES))
+    is_odd = lax.axis_index("wide") % 2 == 1
+    for at, rows, up_value, down_value in (
+        (0, 16, l3_out[0:16, :], l3_out[48:64, :]), (16, 8, l2_out[0:8, :], l2_out[8:16, :]),
+    ):
+        even_out[at : at + rows, :] = jnp.where(is_odd, up_value, down_value)
+        odd_out[at : at + rows, :] = jnp.where(is_odd, down_value, up_value)
+    even_out[24:28, :] = l1_out[0:4, :]
+    odd_out[24:28, :] = l1_out[0:4, :]
 
     for copy in copies:
         copy.wait()
@@ -215,11 +204,12 @@
         up_kernel,
         out_shape=(
             jax.ShapeDtypeStruct((LEAVES, 128), F32), near_memory(64, 128), near_memory(16, 128),
-            near_memory(8, 128), near_memory(16 * CHUNK_WIDE, 128),
+            near_memory(8, 128), near_memory(HALO_ROWS, 128), near_memory(HALO_ROWS, 128),
+            near_memory(128, 128),
             near_memory(2, 512, 256, kind=BF16), near_memory(5, 56, 128), near_memory(5, 56, 128),
         ),
         in_specs=[VMEM, VMEM, VMEM, VMEM, ANY],
-        out_specs=(ANY,) + (VMEM,) * 7,
+        out_specs=(ANY,) + (VMEM,) * 9,
         scratch_shapes=[
             scratch((2, 9 * GROUPS, LANES)),
             scratch((2, 8 * GROUPS, LANES)),
@@ -304,19 +294,12 @@
     return first + pltpu.roll(second, 64, 1)
 
 
-def pack_kernel(l3, l2, l1, got, same, cross, send_out, top, bottom, columns):
-    wide_at = lax.axis_index("wide")
-    narrow_at = lax.axis_index("narrow")
-    above = jnp.maximum(wide_at - 1, 0) * CHUNK_WIDE
-    below = jnp.minimum(wide_at + 1, 15) * CHUNK_WIDE
-    top[0:HALO_ROWS, :] = jnp.where(wide_at > 0, got[pl.ds(above, HALO_ROWS), :], 0.0)
-    bottom[0:HALO_ROWS, :] = jnp.where(wide_at < 15, got[pl.ds(below, HALO_ROWS), :], 0.0)
-    roots = got[pl.ds(HALO_ROWS, 16, stride=CHUNK_WIDE), :]
-    for j in range(8):
-        at = j * CHUNK_NARROW + HALO_ROWS
-        send_out[at : at + 16, :] = roots
-
-    results = []
+def pack_kernel(
+    l3, l2, l1, even, odd, same, cross, even_out, odd_out, top, bottom, columns, west_out, east_out
+):
+    is_odd = lax.axis_index("wide") % 2 == 1
+    top[...] = jnp.where(is_odd, even[...], odd[...])
+    bottom[...] = jnp.where(is_odd, odd[...], even[...])
     for number, (grid, (side, row_at)) in enumerate(zip((l3, l2, l1), LEVELS)):
         level = 4 - number
         for east in range(2):
@@ -329,53 +312,30 @@
                 column[at + 2 + side : at + 4 + side, :] = bottom[pl.ds(row_at + c, 2, stride=side), :]
             for target, dcs in enumerate(((-2, -1), (-3, -2)) if east else ((2, 3), (1, 2))):
                 value = column_products(column, same.at[level], cross.at[level], dcs)
-                results.append((east, row_at + target * side, value[0:side]))
-
-    for east in range(2):
-        @pl.when((narrow_at < 7) if east else (narrow_at > 0))
-        def _():
-            base = (narrow_at + (1 if east else -1)) * CHUNK_NARROW
-            for which, at, value in results:
-                if which == east:
-                    send_out[pl.ds(base + at, value.shape[0]), :] = value
+                out = east_out if east else west_out
+                at = row_at + target * side
+                out[at : at + side, :] = value[0:side]
+    is_odd = lax.axis_index("narrow") % 2 == 1
+    even_out[...] = jnp.where(is_odd, west_out[...], east_out[...])
+    odd_out[...] = jnp.where(is_odd, east_out[...], west_out[...])
 
 
 def pack(*operands):
     return pl.pallas_call(
         pack_kernel,
-        out_shape=(
-            near_memory(8 * CHUNK_NARROW, 128), near_memory(32, 128), near_memory(32, 128),
-        ),
-        in_specs=[VMEM] * 6,
-        out_specs=(VMEM,) * 3,
-        scratch_shapes=[pltpu.VMEM((6, 2 * PITCH, 128), F32)],
+        out_shape=(near_memory(HALO_ROWS, 128),) * 4,
+        in_specs=[VMEM] * 7,
+        out_specs=(VMEM,) * 4,
+        scratch_shapes=[
+            pltpu.VMEM((6, 2 * PITCH, 128), F32), pltpu.VMEM((HALO_ROWS, 128), F32),
+            pltpu.VMEM((HALO_ROWS, 128), F32),
+        ],
         name="pack",
     )(*operands)
 
 
-def down_kernel(
-    l3, l2, l1, top, bottom, got, w_two, same, cross,
-    out0, out1, out2, out3, outc, outt,
-    r3, r2, r1, total, grid, region, xc, xt, coarse,
-):
-    wide_at = lax.axis_index("wide")
-    narrow_at = lax.axis_index("narrow")
-    grid[...] = jnp.zeros_like(grid)
-    for j in range(8):
-        at = j * CHUNK_NARROW + HALO_ROWS
-        grid[pl.ds(3 * PITCH + 3 + j, 16, stride=PITCH), :] = got[at : at + 16, :]
-    for row_bit in range(2):
-        for col_bit in range(2):
-            lanes = slice((2 * row_bit + col_bit) * 128, (2 * row_bit + col_bit + 1) * 128)
-            for r in range(8):
-                at = (2 * r + row_bit + 3) * PITCH + 3 + col_bit
-                xc[4 * r : 4 * r + 4, lanes] = grid[pl.ds(at, 4, stride=2), :]
-    coarse[...] = merge(xc[...], w_two[1])
-    gather_children(coarse, xt, 4, 2)
-    peak = merge(xt[...], w_two[0])
-    for r in range(4):
-        outt[r] = peak[2 * r : 2 * r + 2]
-
+def near_kernel(l3, l2, l1, top, bottom, same, cross, saved, other, r3, r2, r1):
+    other[...] = jnp.zeros_like(other)
     for number, (own, region_k, (side, row_at)) in enumerate(
         zip((l3, l2, l1), (r3, r2, r1), LEVELS)
     ):
@@ -390,18 +350,56 @@
             region_k[at : at + side, :] = bottom[row_at + r * side : row_at + (r + 1) * side, :]
 
         def store(r, value, base=SAVED[number]):
-            total[base + 8 * r : base + 8 * r + 8, :] = value
+            saved[base + 8 * r : base + 8 * r + 8, :] = value
 
         level = 4 - number
         transfer_rows(region_k, same.at[level], cross.at[level], side, 8, store)
-    before = jnp.maximum(narrow_at - 1, 0) * CHUNK_NARROW
-    after = jnp.minimum(narrow_at + 1, 7) * CHUNK_NARROW
+
+
+def near(*operands):
+    tall = lambda rows: pltpu.VMEM((rows, 128), F32)
+    return pl.pallas_call(
+        near_kernel,
+        out_shape=(near_memory(112, 128), near_memory(8, 128)),
+        in_specs=[VMEM] * 7,
+        out_specs=(VMEM,) * 2,
+        scratch_shapes=[tall(12 * PITCH), tall(8 * PITCH), tall(6 * PITCH)],
+        name="near",
+    )(*operands)
+
+
+def down_kernel(
+    saved, even, odd, roots, w_two, same, cross,
+    out0, out1, out2, out3, outc, outt,
+    total, grid, region, xc, xt, coarse, west, east,
+):
+    wide_at = lax.axis_index("wide")
+    narrow_at = lax.axis_index("narrow")
+    grid[...] = jnp.zeros_like(grid)
+    for r in range(16):
+        at = (r + 3) * PITCH + 3
+        grid[at : at + 8, :] = roots[r * 8 : (r + 1) * 8, :]
+    for row_bit in range(2):
+        for col_bit in range(2):
+            lanes = slice((2 * row_bit + col_bit) * 128, (2 * row_bit + col_bit + 1) * 128)
+            for r in range(8):
+                at = (2 * r + row_bit + 3) * PITCH + 3 + col_bit
+                xc[4 * r : 4 * r + 4, lanes] = grid[pl.ds(at, 4, stride=2), :]
+    coarse[...] = merge(xc[...], w_two[1])
+    gather_children(coarse, xt, 4, 2)
+    peak = merge(xt[...], w_two[0])
+    for r in range(4):
+        outt[r] = peak[2 * r : 2 * r + 2]
+
+    is_odd = narrow_at % 2 == 1
+    west[...] = jnp.where(is_odd, even[...], odd[...])
+    east[...] = jnp.where(is_odd, odd[...], even[...])
+    total[...] = saved[...]
     for number, (side, at) in enumerate(LEVELS):
-        for start, there, first in ((before, narrow_at > 0, 0), (after, narrow_at < 7, side - 2)):
+        for given, first in ((west, 0), (east, side - 2)):
             for k in range(2):
-                given = jnp.where(there, got[pl.ds(start + at + k * side, side), :], 0.0)
                 rows = pl.ds(SAVED[number] + first + k, side, stride=8)
-                total[rows, :] = total[rows, :] + given
+                total[rows, :] = total[rows, :] + given[at + k * side : at + (k + 1) * side, :]
     for number, ((side, _), out) in enumerate(zip(LEVELS, (out3, out2, out1))):
         for r in range(side):
             at = SAVED[number] + 8 * r
@@ -444,11 +442,12 @@
             shape(1, 1, 128), shape(2, 2, 128), shape(4, 4, 128), shape(8, 8, 128),
             shape(8, 4, 128), shape(4, 2, 128),
         ),
-        in_specs=[VMEM] * 9,
+        in_specs=[VMEM] * 7,
         out_specs=(VMEM,) * 6,
         scratch_shapes=[
-            tall(12 * PITCH), tall(8 * PITCH), tall(6 * PITCH), tall(112), tall(22 * PITCH), tall(12 * PITCH),
+            tall(112), tall(22 * PITCH), tall(12 * PITCH),
             pltpu.VMEM((32, 512), F32), pltpu.VMEM((8, 512), F32), tall(32),
+            tall(HALO_ROWS), tall(HALO_ROWS),
         ],
         name="downward",
     )(*operands)
@@ -458,21 +457,33 @@
     return lax.all_to_all(boxes[:, None, :], axis, 0, 0, tiled=True)[:, 0, :]
 
 
-def local(offsets, strengths, leaf_map, shift_matrices, transfer_diagonal):
-    leaf, l3, l2, l1, send, w_two, same, cross = upward(
+def swap_pairs(x, axis, first):
+    lower = range(first, lax.axis_size(axis) - 1, 2)
+    pairs = [pair for i in lower for pair in ((i, i + 1), (i + 1, i))]
+    return lax.ppermute(x, axis, pairs)
+
+
+def steps(offsets, strengths, leaf_map, shift_matrices, transfer_diagonal):
+    leaf, l3, l2, l1, even, odd, root, w_two, same, cross = upward(
         offsets.reshape(2, GROUPS, LANES),
         strengths.reshape(2, GROUPS, LANES),
         leaf_map.reshape(GROUPS, LANES),
         transfer_diagonal,
         shift_matrices,
     )
-    l3, l2, l1, got, w_two, same, cross = kept_near(
-        l3, l2, l1, exchange(send, "wide"), w_two, same, cross
+    odd = swap_pairs(odd, "wide", 1)
+    even = swap_pairs(even, "wide", 0)
+    roots = exchange(root, ALL)
+    l3, l2, l1, w_two, same, cross, even, odd = kept_near(
+        l3, l2, l1, w_two, same, cross, even, odd
     )
-    send, top, bottom = pack(l3, l2, l1, got, same, cross)
-    top, bottom, got = kept_near(top, bottom, exchange(send, "narrow"))
+    even, odd, top, bottom = pack(l3, l2, l1, even, odd, same, cross)
+    odd = swap_pairs(odd, "narrow", 1)
+    even = swap_pairs(even, "narrow", 0)
+    top, bottom = kept_near(top, bottom)
+    saved, _ = near(l3, l2, l1, top, bottom, same, cross)
     local_zero, local_one, local_two, local_three, coarse_local, top_grid = downward(
-        l3, l2, l1, top, bottom, got, w_two, same, cross
+        *kept_near(saved, even, odd, roots), w_two, same, cross
     )
     return (
         leaf.reshape(32, 32, 128), local_zero, local_one, local_two, local_three,
@@ -482,7 +493,7 @@
 
 def solution(mesh):
     return jax.shard_map(
-        local,
+        steps,
         mesh=mesh,
         in_specs=(
             P(None, "wide", "narrow", None),

time: 39.3 us -> 38.2 us (0.972)
  the two profiles are of different devices: /device:TPU:0 before, /device:TPU:40 now
where the time goes in v4:
time: 38.2 us; the launch traced here: 38 us
  starting transfers between devices  19.1 us (50%)
  Pallas kernels  10.7 us (28%)
  waiting for transfers between devices  7.56 us (20%)
  between operations  0.68 us (2%)
    all_to_all x1, starting transfers between devices, exchange(): return lax.all_to_all(boxes[:, None, :], axis, 0, 0, tiled=True)[:, 0, :]  10.2 us
    ppermute x4, starting transfers between devices, swap_pairs(): return lax.ppermute(x, axis, pairs)  8.92 us
    pallas_call x1, Pallas kernels, upward(): pl.pallas_call(up_kernel, out_shape=(jax.ShapeDtypeStruct((LEAVES, 128),...  8.72 us
    ppermute x4, waiting for transfers between devices, swap_pairs(): return lax.ppermute(x, axis, pairs)  7.56 us
    pallas_call x1, Pallas kernels, downward(): pl.pallas_call(down_kernel, out_shape=(shape(1, 1, 128), shape(2, 2, 128)...  1.02 us
  transfers between devices with their start and end apart: 5, of which 2 were waited for; matrix products, arithmetic and copies ran while one was open for 0% of the time, Pallas kernels for 2%

profile of v4, /device:TPU:40, one launch (start us, length us, event | category | flops | bytes accessed | tf_op | source)
XLA Modules:
  0.0 38.0 jit_solution(15394664303705942704)
XLA Ops:
  0.6 8.7 %upward.1 = (f32[1024,128]{1,0:T(8,128)}, f32[64,128]{1,0:T(8,128)S(1)}, f32[16,128]{1,0:T(8,128)S(1)}, f32[8,128]{1,0:T(8,128)S(1)}, f32[28,128]{1,0:T(8,128)S(...) custom-call(f32[2,64,128]{2,1,0:T(8,128)} %bitcast.9, ...), custom_call_target="tpu_custom_call" | custom-call | tf_op jit(solution)/shard_map/upward/pallas_call | solution.py:203
  9.4 10.2 %all-to-all-start = ((f32[128,1,128]{2,1,0:T(1,128)}), f32[128,1,128]{2,1,0:T(1,128)S(1)}, u32[]{:S(2)}, u32[]{:S(2)}) async-start(f32[128,1,128]{2,1,0:T(1,128)} %bitcast.5), calls=%async_computation | async-start | bytes 131072 | tf_op jit(solution)/shard_map/all_to_all | solution.py:457
  19.6 0.2 collective-permute-start
  19.8 3.2 %collective-permute-start.1 = (f32[28,128]{1,0:T(8,128)S(1)}, f32[28,128]{1,0:T(8,128)S(1)}, u32[]{:S(2)}, u32[]{:S(2)}) collective-permute-start(f32[28,128]{1,0:T(8,128)S(1)} %get-tuple-element.33), channel_id=1, source_target_pairs={{8,16},{16,8},{24,32},{32,24},{40,48},{48,40},{56,64},{64,56},{72,... | collective-permute-start | bytes 43016 | tf_op jit(solution)/shard_map/ppermute | solution.py:463
  22.9 0.0 collective-permute-done.even
  22.9 2.8 %collective-permute-done.1.odd = f32[28,128]{1,0:T(8,128)S(1)} collective-permute-done((f32[28,128]{1,0:T(8,128)S(1)}, f32[28,128]{1,0:T(8,128)S(1)}, u32[]{:S(2)}, u32[]{:S(2)}) %collective-permute-start.1) | collective-permute-done | bytes 14368 | tf_op jit(solution)/shard_map/ppermute | solution.py:463
  25.7 0.2 pack.1
  25.9 3.1 %collective-permute-start.2 = (f32[28,128]{1,0:T(8,128)S(1)}, f32[28,128]{1,0:T(8,128)S(1)}, u32[]{:S(2)}, u32[]{:S(2)}) collective-permute-start(f32[28,128]{1,0:T(8,128)S(1)} %get-tuple-element.39), channel_id=1, source_target_pairs={{0,1},{1,0},{2,3},{3,2},{4,5},{5,4},{6,7},{7,6},{8,9},{9,8},{10,11... | collective-permute-start | bytes 43016 | tf_op jit(solution)/shard_map/ppermute | solution.py:463
  29.0 2.5 %collective-permute-start.3 = (f32[28,128]{1,0:T(8,128)S(1)}, f32[28,128]{1,0:T(8,128)S(1)}, u32[]{:S(2)}, u32[]{:S(2)}) collective-permute-start(f32[28,128]{1,0:T(8,128)S(1)} %get-tuple-element.40), channel_id=1, source_target_pairs={{1,2},{2,1},{3,4},{4,3},{5,6},{6,5},{9,10},{10,9},{11,12},{12,11},... | collective-permute-start | bytes 43016 | tf_op jit(solution)/shard_map/ppermute | solution.py:463
  31.4 0.7 %near.1 = (f32[112,128]{1,0:T(8,128)S(1)}, f32[8,128]{1,0:T(8,128)}) custom-call(f32[64,128]{1,0:T(8,128)S(1)} %get-tuple-element.29.l3, f32[16,128]{1,0:T(8,128)S(1)} %get-tuple-element.30.l2, f32[8,128]{1,0:T(8,128)S(1)} %get-tuple-element.31.l1, f32[28,128]{1,0:T(8,128)S(1)} %get-tuple-element.36.top, f32[28,128]{1,0:T(8,128)S(1)} %get-tuple-element.37.bottom, ...), custom_call_target="tpu_custom_call" | custom-call | tf_op jit(solution)/shard_map/near/pallas_call | solution.py:361
  32.2 0.0 collective-permute-done.2.even
  32.2 4.8 %collective-permute-done.3.odd = f32[28,128]{1,0:T(8,128)S(1)} collective-permute-done((f32[28,128]{1,0:T(8,128)S(1)}, f32[28,128]{1,0:T(8,128)S(1)}, u32[]{:S(2)}, u32[]{:S(2)}) %collective-permute-start.3) | collective-permute-done | bytes 14368 | tf_op jit(solution)/shard_map/ppermute | solution.py:463
  37.0 0.0 all-to-all-done
  37.0 1.0 %downward.1 = (f32[1,1,128]{2,1,0:T(1,128)}, f32[2,2,128]{2,1,0:T(2,128)}, f32[4,4,128]{2,1,0:T(4,128)}, f32[8,8,128]{2,1,0:T(8,128)}, f32[8,4,128]{2,1,0:T(4,128)}, /*index=5*/f32[4,2,128]{2,1,0:T(2,128)}) custom-call(f32[112,128]{1,0:T(8,128)S(1)} %get-tuple-element.38.saved, f32[28,128]{1,0:T(8,128)S(1)} %collective-permute-done.2.even, ...), custom_call_target="tpu_custom_call" | custom-call | tf_op jit(solution)/shard_map/downward/pallas_call | solution.py:439
Async XLA Ops:
  9.4 27.6 %all-to-all-start = ((f32[128,1,128]{2,1,0:T(1,128)}), f32[128,1,128]{2,1,0:T(1,128)S(1)}, u32[]{:S(2)}, u32[]{:S(2)}) async-start(f32[128,1,128]{2,1,0:T(1,128)} %bitcast.5), calls=%async_computation | async-start | bytes 131072 | tf_op jit(solution)/shard_map/all_to_all | solution.py:457
  19.6 3.4 %collective-permute-start = (f32[28,128]{1,0:T(8,128)S(1)}, f32[28,128]{1,0:T(8,128)S(1)}, u32[]{:S(2)}, u32[]{:S(2)}) collective-permute-start(f32[28,128]{1,0:T(8,128)S(1)} %get-tuple-element.32), channel_id=1, source_target_pairs={{0,8},{8,0},{16,24},{24,16},{32,40},{40,32},{48,56},{56,48},{64,72... | collective-permute-start | bytes 43016 | tf_op jit(solution)/shard_map/ppermute | solution.py:463
  19.8 6.0 %collective-permute-start.1 = (f32[28,128]{1,0:T(8,128)S(1)}, f32[28,128]{1,0:T(8,128)S(1)}, u32[]{:S(2)}, u32[]{:S(2)}) collective-permute-start(f32[28,128]{1,0:T(8,128)S(1)} %get-tuple-element.33), channel_id=1, source_target_pairs={{8,16},{16,8},{24,32},{32,24},{40,48},{48,40},{56,64},{64,56},{72,... | collective-permute-start | bytes 43016 | tf_op jit(solution)/shard_map/ppermute | solution.py:463
  25.9 6.3 %collective-permute-start.2 = (f32[28,128]{1,0:T(8,128)S(1)}, f32[28,128]{1,0:T(8,128)S(1)}, u32[]{:S(2)}, u32[]{:S(2)}) collective-permute-start(f32[28,128]{1,0:T(8,128)S(1)} %get-tuple-element.39), channel_id=1, source_target_pairs={{0,1},{1,0},{2,3},{3,2},{4,5},{5,4},{6,7},{7,6},{8,9},{9,8},{10,11... | collective-permute-start | bytes 43016 | tf_op jit(solution)/shard_map/ppermute | solution.py:463
  29.0 8.0 %collective-permute-start.3 = (f32[28,128]{1,0:T(8,128)S(1)}, f32[28,128]{1,0:T(8,128)S(1)}, u32[]{:S(2)}, u32[]{:S(2)}) collective-permute-start(f32[28,128]{1,0:T(8,128)S(1)} %get-tuple-element.40), channel_id=1, source_target_pairs={{1,2},{2,1},{3,4},{4,3},{5,6},{6,5},{9,10},{10,9},{11,12},{12,11},... | collective-permute-start | bytes 43016 | tf_op jit(solution)/shard_map/ppermute | solution.py:463
